TPU v7x, 128 devices: a whole 4x4x4 slice. The times are simulated.
128 devices in a mesh: row: 16 (over y, z), col: 8 (over x, core).
Axes of the slice: x: 4, y: 4, z: 4, core: 2. Of those that a mesh axis runs over, the one named last changes fastest.
Arguments:
- queries: bfloat16 [49152, 4096], P(('row', 'col')), may hold values from -6 to 6
- keys: bfloat16 [65536, 256], P(('row', 'col')), may hold values from -6 to 6
- values: bfloat16 [65536, 256], P(('row', 'col')), may hold values from -6 to 6
- output_gradient: bfloat16 [49152, 4096], P(('row', 'col')), may hold values from -6 to 6
- tile_block_table: int32 [384, 3], P(('row', 'col')), may hold values from 0 to 127, as said below
Outputs:
- dqueries: bfloat16 [49152, 4096], P(('row', 'col'))
- dkeys: bfloat16 [65536, 256], P(('row', 'col'))
- dvalues: bfloat16 [65536, 256], P(('row', 'col'))
Inputs may be any that keep to these rules, and one draw needn't show every extreme that they name: `tile_block_table`: A tile's first id is the block that holds its own query rows; its 3 ids are distinct and none is larger than that block. Block b is held by the device of index b // 1 in the order row-major over (row, col). The tiles of one device name at most 1 distinct blocks held on devices of one col index, and at most 2 distinct blocks held on devices of one row index.
All inputs are finite; a program needn't handle non-finite values.
Results may differ from a plain program's by a relative error of at most 0.0064.
Values may be sent and summed in bfloat16 or wider, within the bound.
A program may use at most 192 MiB of HBM per device.

v0:
```python
import jax
import jax.numpy as jnp
from jax import lax
from jax.sharding import PartitionSpec as P

QUERY_HEADS = 32
KEY_VALUE_HEADS = 2
HEAD_WIDTH = 128
GROUP_WIDTH = 16
TILE_QUERY_ROWS = 128
BLOCK_KEY_ROWS = 512
PICKED_BLOCKS = 3


def sent_to_all(value, axis):
    copies = jnp.broadcast_to(value, (lax.axis_size(axis), *value.shape))
    return lax.all_to_all(copies, axis, split_axis=0, concat_axis=0, tiled=True)


def joined_along(blocks, dim):
    shape = list(blocks.shape[1:])
    shape[dim] *= blocks.shape[0]
    return jnp.moveaxis(blocks, 0, dim).reshape(shape)


def gather_directly(value, axis, dim):
    blocks = sent_to_all(value, axis)
    return joined_along(blocks, dim)


def pair_grads(
    tile_query_rows, gradient_rows, block_key_rows, block_value_rows, query_place, key_place
):
    factor = HEAD_WIDTH ** (-0.5)
    forward = (((1,), (1,)), ((), ()))
    backward = (((0,), (0,)), ((), ()))
    scores = (
        lax.dot_general(
            tile_query_rows, block_key_rows, forward, preferred_element_type=jnp.float32
        )
        * factor
    )
    scores = jnp.where(key_place[None, :] <= query_place[:, None], scores, -jnp.inf)
    weights = jax.nn.softmax(scores, axis=-1)
    grad_weights = lax.dot_general(
        gradient_rows, block_value_rows, forward, preferred_element_type=jnp.float32
    )
    row_delta = jnp.sum(weights * grad_weights, axis=-1, keepdims=True)
    grad_scores = (weights * (grad_weights - row_delta) * factor).astype(jnp.bfloat16)
    query_gradient = jnp.dot(grad_scores, block_key_rows, preferred_element_type=jnp.float32)
    key_gradient = lax.dot_general(
        grad_scores, tile_query_rows, backward, preferred_element_type=jnp.float32
    )
    value_gradient = lax.dot_general(
        weights.astype(jnp.bfloat16), gradient_rows, backward, preferred_element_type=jnp.float32
    )
    return (query_gradient, key_gradient, value_gradient)


def item_grads(packed):
    query_item, gradient_item, block_item, query_place, key_place = packed
    return pair_grads(
        query_item, gradient_item, block_item[0], block_item[1], query_place, key_place
    )


def local(queries, keys, values, output_gradient, tile_block_table):
    n_row = lax.axis_size("row")
    n_col = lax.axis_size("col")
    my_row = lax.axis_index("row")
    my_col = lax.axis_index("col")
    devices = n_row * n_col
    my_device = my_row * n_col + my_col
    blk_dev = keys.shape[0] // BLOCK_KEY_ROWS
    device_tile_count = tile_block_table.shape[0]
    kv_width = keys.shape[1]
    cap_row = 2 * blk_dev
    nblocks = devices * blk_dev
    band_rows = n_row * blk_dev
    flat_width = BLOCK_KEY_ROWS * 2 * kv_width
    starting_position = nblocks * BLOCK_KEY_ROWS - devices * device_tile_count * TILE_QUERY_ROWS
    catalog = jnp.arange(nblocks, dtype=jnp.int32)
    row_lists = gather_directly(tile_block_table, "col", 0)
    wanted = jnp.any(
        row_lists.reshape(n_col, device_tile_count * PICKED_BLOCKS, 1) == catalog, axis=1
    ).astype(jnp.int32)
    layout = wanted.reshape(n_col, n_row, n_col, blk_dev)
    by_col = jnp.transpose(layout, (0, 2, 1, 3)).reshape(n_col, n_col, band_rows)
    col_rank = jnp.cumsum(by_col, axis=2) - by_col
    local_kv = jnp.concatenate((keys, values), axis=1)
    column = lax.all_gather(local_kv, "row", axis=0, tiled=True).reshape(band_rows, flat_width)
    row_wants = by_col[:, my_col, :]
    row_ranks = col_rank[:, my_col, :]
    slot_ids = jnp.arange(blk_dev, dtype=jnp.int32)
    picker = (row_ranks[:, None, :] == slot_ids[None, :, None]) & (row_wants[:, None, :] == 1)
    picker = picker.astype(jnp.bfloat16).reshape(n_col * blk_dev, band_rows)
    outgoing = jnp.dot(picker, column, preferred_element_type=jnp.float32).astype(jnp.bfloat16)
    landed_parts = lax.all_to_all(
        outgoing.reshape(n_col, blk_dev, flat_width), "col", split_axis=0, concat_axis=0, tiled=True
    )
    landed_parts = landed_parts.reshape(n_col * blk_dev, BLOCK_KEY_ROWS, 2 * kv_width)
    my_lists = tile_block_table.reshape(device_tile_count * PICKED_BLOCKS)
    holder = my_lists // blk_dev
    holder_row = holder // n_col
    holder_col = holder % n_col
    within = my_lists % blk_dev
    my_ranks = col_rank[my_col]
    paired_position = holder_col * blk_dev + my_ranks[holder_col, holder_row * blk_dev + within]
    paired_key_value = jnp.take(landed_parts, paired_position, axis=0).reshape(
        device_tile_count, PICKED_BLOCKS * BLOCK_KEY_ROWS, 2, KEY_VALUE_HEADS, HEAD_WIDTH
    )
    entry_count = device_tile_count * KEY_VALUE_HEADS
    tile_query_rows = queries.reshape(
        device_tile_count, TILE_QUERY_ROWS, KEY_VALUE_HEADS, GROUP_WIDTH, HEAD_WIDTH
    ).transpose(0, 2, 3, 1, 4)
    tile_query_rows = tile_query_rows.reshape(
        entry_count, GROUP_WIDTH * TILE_QUERY_ROWS, HEAD_WIDTH
    )
    gradient_rows = output_gradient.reshape(
        device_tile_count, TILE_QUERY_ROWS, KEY_VALUE_HEADS, GROUP_WIDTH, HEAD_WIDTH
    ).transpose(0, 2, 3, 1, 4)
    gradient_rows = gradient_rows.reshape(entry_count, GROUP_WIDTH * TILE_QUERY_ROWS, HEAD_WIDTH)
    block_rows = paired_key_value.transpose(0, 3, 2, 1, 4).reshape(
        entry_count, 2, PICKED_BLOCKS * BLOCK_KEY_ROWS, HEAD_WIDTH
    )
    global_tile_index = my_device * device_tile_count + jnp.arange(
        device_tile_count, dtype=jnp.int32
    )
    rows_per_head = jnp.arange(GROUP_WIDTH * TILE_QUERY_ROWS, dtype=jnp.int32) % TILE_QUERY_ROWS
    query_place = jnp.repeat(
        starting_position + global_tile_index[:, None] * TILE_QUERY_ROWS + rows_per_head[None, :],
        KEY_VALUE_HEADS,
        axis=0,
    )
    row_offsets = jnp.arange(BLOCK_KEY_ROWS, dtype=jnp.int32)
    key_place = jnp.repeat(
        (tile_block_table[:, :, None] * BLOCK_KEY_ROWS + row_offsets).reshape(
            device_tile_count, PICKED_BLOCKS * BLOCK_KEY_ROWS
        ),
        KEY_VALUE_HEADS,
        axis=0,
    )
    query_gradient, key_gradient, value_gradient = lax.map(
        item_grads, (tile_query_rows, gradient_rows, block_rows, query_place, key_place)
    )
    dqueries = query_gradient.reshape(
        device_tile_count, KEY_VALUE_HEADS, GROUP_WIDTH, TILE_QUERY_ROWS, HEAD_WIDTH
    ).transpose(0, 3, 1, 2, 4)
    dqueries = dqueries.reshape(
        device_tile_count * TILE_QUERY_ROWS, QUERY_HEADS * HEAD_WIDTH
    ).astype(jnp.bfloat16)
    paired_terms = jnp.stack((key_gradient, value_gradient), axis=0).reshape(
        2, device_tile_count, KEY_VALUE_HEADS, PICKED_BLOCKS, BLOCK_KEY_ROWS, HEAD_WIDTH
    )
    paired_terms = paired_terms.transpose(1, 3, 4, 0, 2, 5).reshape(
        device_tile_count * PICKED_BLOCKS, flat_width
    )
    row_span = n_col * blk_dev
    col_lists = gather_directly(tile_block_table, "row", 0)
    col_wanted = jnp.any(
        col_lists.reshape(n_row, device_tile_count * PICKED_BLOCKS, 1) == catalog, axis=1
    ).astype(jnp.int32)
    by_row = col_wanted.reshape(n_row, n_row, row_span)
    row_rank = jnp.cumsum(by_row, axis=2) - by_row
    own_ranks = row_rank[my_row]
    row_slot = holder_row * cap_row + own_ranks[holder_row, holder_col * blk_dev + within]
    slot_count = n_row * cap_row
    assign = (row_slot[None, :] == jnp.arange(slot_count, dtype=jnp.int32)[:, None]).astype(
        jnp.float32
    )
    partials = jnp.dot(
        assign, paired_terms, precision=lax.Precision.HIGHEST, preferred_element_type=jnp.float32
    ).astype(jnp.bfloat16)
    returned = lax.all_to_all(
        partials.reshape(n_row, cap_row, flat_width), "row", split_axis=0, concat_axis=0, tiled=True
    )
    returned = returned.reshape(slot_count, flat_width)
    sender_wants = by_row[:, my_row, :]
    sender_ranks = row_rank[:, my_row, :]
    row_slot_ids = jnp.arange(cap_row, dtype=jnp.int32)
    collect = (sender_ranks[:, None, :] == row_slot_ids[None, :, None]) & (
        sender_wants[:, None, :] == 1
    )
    collect = collect.astype(jnp.bfloat16).reshape(slot_count, row_span).T
    result = lax.psum_scatter(
        jnp.dot(collect, returned, preferred_element_type=jnp.float32),
        "col",
        scatter_dimension=0,
        tiled=True,
    )
    result = result.reshape(blk_dev * BLOCK_KEY_ROWS, 2 * kv_width)
    return (
        dqueries,
        result[:, :kv_width].astype(jnp.bfloat16),
        result[:, kv_width:].astype(jnp.bfloat16),
    )


def solution(mesh):
    return jax.shard_map(
        local,
        mesh=mesh,
        in_specs=(
            P(("row", "col"), None),
            P(("row", "col"), None),
            P(("row", "col"), None),
            P(("row", "col"), None),
            P(("row", "col"), None),
        ),
        out_specs=(P(("row", "col"), None), P(("row", "col"), None), P(("row", "col"), None)),
        check_vma=False,
    )
```

profile of v0, /device:TPU:0, one launch (start us, length us, event | category | flops | bytes accessed | tf_op | source)
XLA Modules:
  0.0 970.5 jit_solution(15433184357276598834)
XLA Ops:
  10.4 4.4 all-to-all-start
  14.8 5.4 all-to-all-done
  21.5 8.0 all-to-all-start.2
  31.6 52.8 %all-gather.2.cloned.1.call-done = bf16[8192,512]{1,0:T(8,128)(2,1)} async-done(((bf16[512,512]{1,0:T(8,128)(2,1)}), bf16[8192,512]{1,0:T(8,128)(2,1)}) %all-gather.2.cloned.1.call-update) | async-done | bytes 8388624 | tf_op jit(solution)/shard_map/all_gather | solution.py:91
  84.4 8.0 reshape.350
  92.4 6.6 fusion.27
  99.5 6.3 reduce.7
  105.7 8.0 reshape.390
  113.8 5.0 all-to-all-start.1
  128.7 39.8 %all-to-all-done.1 = bf16[8,2,131072]{2,1,0:T(2,128)(2,1)} async-done(((bf16[8,2,131072]{2,1,0:T(2,128)(2,1)}), bf16[8,2,131072]{2,1,0:T(2,128)(2,1)}, u32[]{:S(2)}, u32[]{:S(2)}) %all-to-all-start.1) | async-done | bytes 4194336 | tf_op jit(solution)/shard_map/all_to_all | solution.py:98
  168.4 8.8 reshape.391
  177.2 26.5 %reduce.2 = bf16[8,262144]{1,0:T(8,128)(2,1)} reduce(bf16[8,1,262144]{2,1,0:T(2,128)(2,1)} %reshape.391, bf16[]{:T(256)} %constant.181), dimensions={1}, to_apply=%all_to_all.13.reduce_sub_computation | reduce | bytes 8388610 | tf_op jit(solution)/shard_map/all_to_all | solution.py:98
  203.7 5.5 copy.115
  209.2 5.7 gather_fusion.1
  215.0 7.8 gather.20
  222.8 11.5 %fusion.29 = bf16[3,2,2,1536,128]{4,1,2,3,0:T(2,128)(2,1)S(1)} fusion(bf16[3,1536,2,2,128]{4,3,2,1,0:T(2,128)(2,1)} %gather.20, pred[3,1536]{1,0:T(4,128)(4,1)S(1)} %bitcast.152), kind=kLoop, calls=%fused_computation.42 | loop fusion | flops 2359296 | bytes 9441792 | tf_op jit(solution)/shard_map/transpose | solution.py:123
  237.2 227.4 %while.14 = (s32[]{:T(128)}, bf16[6,2048,128]{2,1,0:T(8,128)(2,1)}, f32[6,1536,128]{2,1,0:T(8,128)}, f32[6,1536,128]{2,1,0:T(8,128)}, s32[6,1536]{1,0:T(8,128)S(...) while((s32[]{:T(128)}, bf16[6,2048,128]{2,1,0:T(8,128)(2,1)}, ...), condition=%wide.region_6.7_spmd, body=%wide.region_2.6_spmd.sunk | while | flops 4086294528 | bytes 213654736 | solution.py:143
  248.4 10.5 %multiply_reduce_fusion.2 = (f32[2048]{0:T(1024)S(1)}, f32[2048,1536]{0,1:T(8,128)}) fusion(f32[2048]{0:T(1024)S(1)} %fusion.73, f32[2048,1536]{0,1:T(8,128)} %copy-done, f32[2048]{0:T(1024)S(1)} %get-tuple-element.142, bf16[6,2,1536,128]{3,2,1,0:T(8,128)(2,1)} %get-tuple-element.176, s32[]{:T(128)} %get-tuple-element.157, s32[]{:T(128)S(6)} %add.285, ...), kind=kOutput, calls=%fused_computation.4.clone.1 | convolution fusion | flops 817887232 | bytes 26108932 | tf_op jit(solution)/shard_map/while/body/eval_jaxpr/dot_general | solution.py:45
  261.1 6.7 multiply_convert_fusion.2
  267.8 3.8 fusion.75
  271.6 3.7 fusion.74
  286.3 10.5 %multiply_reduce_fusion.2 = (f32[2048]{0:T(1024)S(1)}, f32[2048,1536]{0,1:T(8,128)}) fusion(f32[2048]{0:T(1024)S(1)} %fusion.73, f32[2048,1536]{0,1:T(8,128)} %copy-done, f32[2048]{0:T(1024)S(1)} %get-tuple-element.142, bf16[6,2,1536,128]{3,2,1,0:T(8,128)(2,1)} %get-tuple-element.176, s32[]{:T(128)} %get-tuple-element.157, s32[]{:T(128)S(6)} %add.285, ...), kind=kOutput, calls=%fused_computation.4.clone.1 | convolution fusion | flops 817887232 | bytes 26108932 | tf_op jit(solution)/shard_map/while/body/eval_jaxpr/dot_general | solution.py:45
  298.9 6.7 multiply_convert_fusion.2
  305.6 3.8 fusion.75
  324.1 10.5 %multiply_reduce_fusion.2 = (f32[2048]{0:T(1024)S(1)}, f32[2048,1536]{0,1:T(8,128)}) fusion(f32[2048]{0:T(1024)S(1)} %fusion.73, f32[2048,1536]{0,1:T(8,128)} %copy-done, f32[2048]{0:T(1024)S(1)} %get-tuple-element.142, bf16[6,2,1536,128]{3,2,1,0:T(8,128)(2,1)} %get-tuple-element.176, s32[]{:T(128)} %get-tuple-element.157, s32[]{:T(128)S(6)} %add.285, ...), kind=kOutput, calls=%fused_computation.4.clone.1 | convolution fusion | flops 817887232 | bytes 26108932 | tf_op jit(solution)/shard_map/while/body/eval_jaxpr/dot_general | solution.py:45
  336.8 6.7 multiply_convert_fusion.2
  343.4 3.8 fusion.75
  361.9 10.5 %multiply_reduce_fusion.2 = (f32[2048]{0:T(1024)S(1)}, f32[2048,1536]{0,1:T(8,128)}) fusion(f32[2048]{0:T(1024)S(1)} %fusion.73, f32[2048,1536]{0,1:T(8,128)} %copy-done, f32[2048]{0:T(1024)S(1)} %get-tuple-element.142, bf16[6,2,1536,128]{3,2,1,0:T(8,128)(2,1)} %get-tuple-element.176, s32[]{:T(128)} %get-tuple-element.157, s32[]{:T(128)S(6)} %add.285, ...), kind=kOutput, calls=%fused_computation.4.clone.1 | convolution fusion | flops 817887232 | bytes 26108932 | tf_op jit(solution)/shard_map/while/body/eval_jaxpr/dot_general | solution.py:45
  374.6 6.7 multiply_convert_fusion.2
  381.2 3.8 fusion.75
  399.7 10.5 %multiply_reduce_fusion.2 = (f32[2048]{0:T(1024)S(1)}, f32[2048,1536]{0,1:T(8,128)}) fusion(f32[2048]{0:T(1024)S(1)} %fusion.73, f32[2048,1536]{0,1:T(8,128)} %copy-done, f32[2048]{0:T(1024)S(1)} %get-tuple-element.142, bf16[6,2,1536,128]{3,2,1,0:T(8,128)(2,1)} %get-tuple-element.176, s32[]{:T(128)} %get-tuple-element.157, s32[]{:T(128)S(6)} %add.285, ...), kind=kOutput, calls=%fused_computation.4.clone.1 | convolution fusion | flops 817887232 | bytes 26108932 | tf_op jit(solution)/shard_map/while/body/eval_jaxpr/dot_general | solution.py:45
  412.3 6.7 multiply_convert_fusion.2
  419.0 3.8 fusion.75
  437.5 10.5 %multiply_reduce_fusion.2 = (f32[2048]{0:T(1024)S(1)}, f32[2048,1536]{0,1:T(8,128)}) fusion(f32[2048]{0:T(1024)S(1)} %fusion.73, f32[2048,1536]{0,1:T(8,128)} %copy-done, f32[2048]{0:T(1024)S(1)} %get-tuple-element.142, bf16[6,2,1536,128]{3,2,1,0:T(8,128)(2,1)} %get-tuple-element.176, s32[]{:T(128)} %get-tuple-element.157, s32[]{:T(128)S(6)} %add.285, ...), kind=kOutput, calls=%fused_computation.4.clone.1 | convolution fusion | flops 817887232 | bytes 26108932 | tf_op jit(solution)/shard_map/while/body/eval_jaxpr/dot_general | solution.py:45
  450.1 6.7 multiply_convert_fusion.2
  456.8 3.8 fusion.75
  464.6 6.0 copy.97
  470.6 6.0 copy.98
  476.6 5.5 maximum_bitcast_fusion
  482.1 22.1 %reshape.357 = f32[9,262144]{1,0:T(8,128)} reshape(f32[3,3,512,2,2,128]{5,4,3,2,1,0:T(2,128)} %maximum_bitcast_fusion) | data formatting | bytes 18874368 | tf_op jit(solution)/shard_map/reshape | solution.py:155
  504.2 23.0 %convolution_convert_fusion = bf16[32,262144]{1,0:T(8,128)(2,1)} fusion(f32[9,262144]{1,0:T(8,128)} %reshape.357, s32[9]{0:T(128)S(1)} %copy-done.7), kind=kOutput, calls=%fused_computation.35 | convolution fusion | flops 914358528 | bytes 26214436 | tf_op jit(solution)/shard_map/dot_general | solution.py:171
  527.3 16.2 %reshape.358 = bf16[16,2,262144]{2,1,0:T(2,128)(2,1)} reshape(bf16[32,262144]{1,0:T(8,128)(2,1)} %convolution_convert_fusion) | data formatting | bytes 33554432 | tf_op jit(solution)/shard_map/reshape | solution.py:175
  543.5 5.5 all-to-all-start.3
  551.0 3.9 copy.116
  558.3 283.0 %all-to-all-done.3 = bf16[16,2,262144]{2,1,0:T(2,128)(2,1)} async-done(((bf16[16,2,262144]{2,1,0:T(2,128)(2,1)}), bf16[16,2,262144]{2,1,0:T(2,128)(2,1)}, u32[]{:S(2)}, u32[]{:S(2)}) %all-to-all-start.3) | async-done | bytes 16777248 | tf_op jit(solution)/shard_map/all_to_all | solution.py:174
  841.3 18.1 %convolution_bitcast_fusion.2 = f32[8,262144]{1,0:T(8,128)} fusion(bf16[16,2,262144]{2,1,0:T(2,128)(2,1)} %all-to-all-done.3, s32[16,8]{0,1:T(8,128)S(1)} %dynamic-slice_bitcast_fusion.5, pred[16,8]{0,1:T(8,128)(4,1)S(1)} %fusion.41), kind=kOutput, calls=%fused_computation.36 | convolution fusion | flops 134218240 | bytes 25166464 | tf_op jit(solution)/shard_map/dot_general | solution.py:186
  859.4 90.5 %all-reduce.2 = bf16[8,262144]{1,0:T(8,128)(2,1)} all-reduce(f32[8,262144]{1,0:T(8,128)} %convolution_bitcast_fusion.2), channel_id=2, replica_groups=mesh['row'=16,'col'=8] {'col'}, use_global_device_ids=true, to_apply=%region_9.10.clone | all-reduce | flops 2097152 | bytes 12582912
  949.9 12.1 %fusion.30 = bf16[262144]{0:T(1024)(128)(2,1)S(1)} fusion(bf16[8,262144]{1,0:T(8,128)(2,1)} %all-reduce.2, u32[]{:T(128)} %bitcast.35), kind=kLoop, calls=%fused_computation.46 | loop fusion | bytes 1048580 | tf_op jit(solution)/shard_map/convert.3
  (140 shorter events, 123.7 us)
Async XLA Ops:
  7.2 77.2 %all-gather.2.cloned.1.call-start = ((), (), s32[]{:S(2)}) async-start(), calls=%async_computation.4 | async-start | bytes 8912896 | tf_op jit(solution)/shard_map/all_gather | solution.py:91
  10.4 9.8 %all-to-all-start = ((s32[8,3,3]{2,1,0:T(4,128)}), s32[8,3,3]{2,1,0:T(4,128)S(1)}, u32[]{:S(2)}, u32[]{:S(2)}) async-start(s32[8,3,3]{2,1,0:T(4,128)} %broadcast_in_dim.65), calls=%async_computation | async-start | bytes 32768 | tf_op jit(solution)/shard_map/all_to_all | solution.py:17
  21.5 92.3 %all-to-all-start.2 = ((s32[16,3,3]{2,1,0:T(4,128)}), s32[16,3,3]{2,1,0:T(4,128)S(1)}, u32[]{:S(2)}, u32[]{:S(2)}) async-start(s32[16,3,3]{2,1,0:T(4,128)} %broadcast_in_dim.70), calls=%async_computation.2 | async-start | bytes 65536 | tf_op jit(solution)/shard_map/all_to_all | solution.py:17
  113.7 5.1 copy-start.6
  113.8 5.4 copy-start.2
  113.8 54.7 %all-to-all-start.1 = ((bf16[8,2,131072]{2,1,0:T(2,128)(2,1)}), bf16[8,2,131072]{2,1,0:T(2,128)(2,1)}, u32[]{:S(2)}, u32[]{:S(2)}) async-start(bf16[8,2,131072]{2,1,0:T(2,128)(2,1)} %reshape.390), calls=%async_computation.1 | async-start | bytes 8388608 | tf_op jit(solution)/shard_map/all_to_all | solution.py:98
  119.2 2.1 copy-start.3
  126.5 50.7 %copy-start.4 = (s32[16,128]{0,1:T(8,128)}, s32[16,128]{0,1:T(8,128)S(1)}, u32[]{:S(2)}) copy-start(s32[16,128]{0,1:T(8,128)S(1)} %copy.95) | copy-start | bytes 24580
  126.6 0.6 copy-start.5
  240.9 4.6 copy-start
  248.4 12.7 %copy-start.1 = (f32[2048,1536]{0,1:T(8,128)S(1)}, f32[2048,1536]{0,1:T(8,128)}, u32[]{:S(2)}) copy-start(f32[2048,1536]{0,1:T(8,128)} %copy-done) | copy-start | bytes 37748740 | tf_op jit(solution)/shard_map/while
  278.7 4.6 copy-start
  286.3 12.7 %copy-start.1 = (f32[2048,1536]{0,1:T(8,128)S(1)}, f32[2048,1536]{0,1:T(8,128)}, u32[]{:S(2)}) copy-start(f32[2048,1536]{0,1:T(8,128)} %copy-done) | copy-start | bytes 37748740 | tf_op jit(solution)/shard_map/while
  316.5 4.6 copy-start
  324.1 12.7 %copy-start.1 = (f32[2048,1536]{0,1:T(8,128)S(1)}, f32[2048,1536]{0,1:T(8,128)}, u32[]{:S(2)}) copy-start(f32[2048,1536]{0,1:T(8,128)} %copy-done) | copy-start | bytes 37748740 | tf_op jit(solution)/shard_map/while
  354.3 4.6 copy-start
  361.9 12.7 %copy-start.1 = (f32[2048,1536]{0,1:T(8,128)S(1)}, f32[2048,1536]{0,1:T(8,128)}, u32[]{:S(2)}) copy-start(f32[2048,1536]{0,1:T(8,128)} %copy-done) | copy-start | bytes 37748740 | tf_op jit(solution)/shard_map/while
  392.1 4.6 copy-start
  399.7 12.7 %copy-start.1 = (f32[2048,1536]{0,1:T(8,128)S(1)}, f32[2048,1536]{0,1:T(8,128)}, u32[]{:S(2)}) copy-start(f32[2048,1536]{0,1:T(8,128)} %copy-done) | copy-start | bytes 37748740 | tf_op jit(solution)/shard_map/while
  429.9 4.6 copy-start
  437.5 12.7 %copy-start.1 = (f32[2048,1536]{0,1:T(8,128)S(1)}, f32[2048,1536]{0,1:T(8,128)}, u32[]{:S(2)}) copy-start(f32[2048,1536]{0,1:T(8,128)} %copy-done) | copy-start | bytes 37748740 | tf_op jit(solution)/shard_map/while
  482.1 22.1 %copy-start.7 = (s32[9]{0:T(128)S(1)}, s32[9]{0:T(128)}, u32[]{:S(2)}) copy-start(s32[9]{0:T(128)} %multiply_add_fusion) | copy-start | bytes 112
  543.5 5.5 copy-start.8
  543.5 297.8 %all-to-all-start.3 = ((bf16[16,2,262144]{2,1,0:T(2,128)(2,1)}), bf16[16,2,262144]{2,1,0:T(2,128)(2,1)}, u32[]{:S(2)}, u32[]{:S(2)}) async-start(bf16[16,2,262144]{2,1,0:T(2,128)(2,1)} %reshape.358), calls=%async_computation.3 | async-start | bytes 33554432 | tf_op jit(solution)/shard_map/all_to_all | solution.py:174
Sparse Core Ops, SparseCore 0:
  10.7 73.6 all-gather.1
where the time goes:
time: 984 us; the launch traced here: 970 us
  waiting for transfers between devices  381 us (39%)
  matrix products  194 us (20%)
  local copies, waits for them, and re-layouts  161 us (16%)
  other arithmetic  106 us (11%)
  blocking collectives  90.5 us (9%)
  starting transfers between devices  23.1 us (2%)
  between operations  14.8 us (2%)
    all_to_all x1, waiting for transfers between devices, local(): lax.all_to_all(partials.reshape(n_row, cap_row, flat_width), 'row', split...  283 us
    unnamed x1, blocking collectives  90.5 us
    dot_general x6, matrix products, pair_grads(): lax.dot_general(gradient_rows, block_value_rows, forward, preferred_eleme...  62.7 us
    all_gather x1, waiting for transfers between devices, local(): lax.all_gather(local_kv, 'row', axis=0, tiled=True)  52.8 us
    convert_element_type x6, other arithmetic, pair_grads(): (weights * (grad_weights - row_delta) * factor).astype(jnp.bfloat16)  39.9 us
    all_to_all x1, waiting for transfers between devices, local(): lax.all_to_all(outgoing.reshape(n_col, blk_dev, flat_width), 'col', split...  39.8 us
    while x24, local copies, waits for them, and re-layouts  29.6 us
    all_to_all x1, other arithmetic, local(): lax.all_to_all(outgoing.reshape(n_col, blk_dev, flat_width), 'col', split...  26.5 us
  transfers between devices with their start and end apart: 5, of which 4 were waited for; matrix products, arithmetic and copies ran while one was open for 5% of the time, Pallas kernels for 0%

commit v1 on v0

v1 whole, which is shorter than its diff:
```python
import functools
import jax, jax.numpy as jnp
from jax import lax
from jax.experimental import pallas as pl
from jax.experimental.pallas import tpu as pltpu
HC=4
NT=(((1,),(1,)),((),()))
NN=(((1,),(0,)),((),()))
F32=jnp.float32; BF=jnp.bfloat16
def attn_kernel(hc, info, q_ref, do_ref, k_ref, v_ref, dq_ref, part_ref, acc):
    tile=pl.program_id(1)
    scale=128**-0.5
    c=scale*1.4426950408889634
    rows=hc*128
    @pl.when(tile==0)
    def _():
        acc[...]=jnp.zeros_like(acc)
    diag=info[18+tile]*128
    slots=[info[tile*3+j] for j in range(3)]
    def chunk(ci,_):
        off=pl.multiple_of(ci*rows,rows)
        q2=q_ref[:,pl.ds(off,rows)]; d2=do_ref[:,pl.ds(off,rows)]
        q=jnp.concatenate([q2[:,h*128:(h+1)*128] for h in range(hc)],axis=0)
        d=jnp.concatenate([d2[:,h*128:(h+1)*128] for h in range(hc)],axis=0)
        ks=[k_ref[slots[j]] for j in range(3)]
        vs=[v_ref[slots[j]] for j in range(3)]
        s=[lax.dot_general(q,ks[j],NT,preferred_element_type=F32) for j in range(3)]
        r=lax.broadcasted_iota(jnp.int32,(rows,512),0)&127
        col=lax.broadcasted_iota(jnp.int32,(rows,512),1)
        s[0]=jnp.where(col<=r+diag,s[0],-jnp.inf)
        m=jnp.max(jnp.maximum(jnp.maximum(s[0],s[1]),s[2]),axis=1,keepdims=True)*c
        p=[jnp.exp2(x*c-m) for x in s]
        l=jnp.sum(p[0]+p[1]+p[2],axis=1,keepdims=True)
        dp=[lax.dot_general(d,vs[j],NT,preferred_element_type=F32) for j in range(3)]
        t=jnp.sum(p[0]*dp[0]+p[1]*dp[1]+p[2]*dp[2],axis=1,keepdims=True)
        inv=1.0/l
        delta=t*inv
        ds=[(p[j]*(dp[j]-delta)).astype(BF) for j in range(3)]
        pb=[p[j].astype(BF) for j in range(3)]
        dq=sum(lax.dot_general(ds[j],ks[j],NN,preferred_element_type=F32) for j in range(3))
        dq=(dq*(inv*scale)).astype(BF)
        for h in range(hc):
            dq_ref[:,pl.ds(off+h*128,128)]=dq[h*128:(h+1)*128]
        qT=(q.astype(F32)*(inv*scale)).astype(BF).T
        dT=(d.astype(F32)*inv).astype(BF).T
        for j in range(3):
            acc[tile*3+j,0]+=lax.dot_general(qT,ds[j],NN,preferred_element_type=F32)
            acc[tile*3+j,1]+=lax.dot_general(dT,pb[j],NN,preferred_element_type=F32)
        return 0
    lax.fori_loop(0,16//hc,chunk,0)
    @pl.when(tile==2)
    def _():
        for sl in range(8):
            i0=info[24+sl]; i1=info[32+sl]; i2=info[40+sl]
            for kv in range(2):
                part_ref[sl,0,kv]=(acc[i0,kv]+acc[i1,kv]+acc[i2,kv]).astype(BF)
def make_info(table, my_device):
    slots=table%8
    tiles=my_device*3+jnp.arange(3,dtype=jnp.int32)
    hit=slots[:,None,:]==jnp.arange(8,dtype=jnp.int32)[None,:,None]
    ent=jnp.arange(9,dtype=jnp.int32).reshape(3,1,3)
    idx=jnp.min(jnp.where(hit,ent,9),axis=2)
    return jnp.concatenate([slots.reshape(9),jnp.zeros(9,jnp.int32),tiles%4,jnp.zeros(3,jnp.int32),idx.reshape(24)])
def attend(q,do,kv,info,hc=HC):
    return pl.pallas_call(
        functools.partial(attn_kernel,hc),
        grid_spec=pltpu.PrefetchScalarGridSpec(num_scalar_prefetch=1,grid=(2,3),
            in_specs=[pl.BlockSpec((128,2048),lambda g,t,_:(t,g)),
                      pl.BlockSpec((128,2048),lambda g,t,_:(t,g)),
                      pl.BlockSpec((None,8,512,128),lambda g,t,_:(2*g,0,0,0)),
                      pl.BlockSpec((None,8,512,128),lambda g,t,_:(2*g+1,0,0,0))],
            out_specs=[pl.BlockSpec((128,2048),lambda g,t,_:(t,g)),
                       pl.BlockSpec((8,1,2,128,512),lambda g,t,_:(0,g,0,0,0))],
            scratch_shapes=[pltpu.VMEM((10,2,128,512),F32)]),
        out_shape=[jax.ShapeDtypeStruct((384,4096),BF),jax.ShapeDtypeStruct((8,2,2,128,512),BF)],
        compiler_params=pltpu.CompilerParams(dimension_semantics=("arbitrary","arbitrary"),vmem_limit_bytes=60*2**20),
        cost_estimate=pl.CostEstimate(flops=24_000_000_000,bytes_accessed=20_000_000,transcendentals=19_000_000),
        name="attend",
    )(info,q,do,kv,kv)
BF=jnp.bfloat16; F32=jnp.float32
MESH=pl.DeviceIdType.MESH
OFFS=(0,-1,1,2)

class Place:
    def __init__(self):
        self.row=lax.axis_index("row"); self.col=lax.axis_index("col")
        self.y=self.row//4; self.z=self.row%4; self.x=self.col//2; self.core=self.col%2
    def rowid(self,first,da,db):
        dy,dz=(db,da) if first=="z" else (da,db)
        return ((self.y+dy+4)%4)*4+(self.z+dz+4)%4
    def colid(self,dx,core):
        return ((self.x+dx+4)%4)*2+core
    def barrier(self):
        sem=pltpu.get_barrier_semaphore()
        for d in (1,2,3,4,5,6,7):
            pl.semaphore_signal(sem,inc=1,device_id={"col":(self.col+d)%8},device_id_type=MESH)
        for dy,dz in ((1,0),(-1,0),(0,1),(0,-1)):
            pl.semaphore_signal(sem,inc=1,device_id={"row":((self.y+dy+4)%4)*4+(self.z+dz+4)%4},device_id_type=MESH)
        pl.semaphore_wait(sem,11)

class Wires:
    def __init__(self,ssem,rsem):
        self.ssem=ssem; self.rsem=rsem; self.pending=[]
    def send(self,src,dst,si,ri,where):
        d=pltpu.make_async_remote_copy(src_ref=src,dst_ref=dst,send_sem=self.ssem.at[si],recv_sem=self.rsem.at[ri],device_id=where,device_id_type=MESH)
        d.start(); self.pending.append(d)
    def got(self,dst,ri,where):
        pltpu.make_async_remote_copy(src_ref=dst,dst_ref=dst,send_sem=self.ssem.at[0],recv_sem=self.rsem.at[ri],device_id=where,device_id_type=MESH).wait_recv()
    def drain(self):
        for d in self.pending: d.wait_send()
        self.pending=[]

AG_SEMS=20
def gather_steps(me,w,own,buf,lo,n,first,base):
    full=pl.ds(lo,n); h0=pl.ds(lo,n//2); h1=pl.ds(lo+n//2,n//2)
    def at(da,db): return {"row":me.rowid(first,da,db)}
    def spread(o,src,dst):
        w.send(src,dst,base+4+o*4,base+4+o*4,at(0,1))
        w.send(src,dst,base+5+o*4,base+5+o*4,at(0,-1))
    def piece(da,db,rows): return buf.at[me.rowid(first,da,db),rows]
    def s0():
        w.send(own,piece(0,0,full),base,base,at(1,0))
        w.send(own,piece(0,0,full),base+1,base+1,at(-1,0))
        spread(0,own,piece(0,0,full))
    def s1():
        w.got(piece(-1,0,full),base,at(-1,0))
        w.send(piece(-1,0,h0),piece(-1,0,h0),base+2,base+2,at(1,0))
        spread(1,piece(-1,0,full),piece(-1,0,full))
        w.got(piece(1,0,full),base+1,at(1,0))
        w.send(piece(1,0,h1),piece(1,0,h1),base+3,base+3,at(-1,0))
        spread(2,piece(1,0,full),piece(1,0,full))
    def turn(o):
        da=OFFS[o]; b=base+4+o*4
        w.got(piece(da,-1,full),b,at(0,-1))
        w.send(piece(da,-1,h0),piece(da,-1,h0),b+2,b+2,at(0,1))
        w.got(piece(da,1,full),b+1,at(0,1))
        w.send(piece(da,1,h1),piece(da,1,h1),b+3,b+3,at(0,-1))
    def s2(): turn(0)
    def s3():
        w.got(piece(2,0,h0),base+2,at(-1,0))
        w.got(piece(2,0,h1),base+3,at(1,0))
        spread(3,piece(2,0,full),piece(2,0,full))
    def s4(): turn(1); turn(2)
    def s5(): turn(3)
    def s6():
        for o in range(4):
            b=base+4+o*4
            w.got(piece(OFFS[o],2,h0),b+2,at(0,-1))
            w.got(piece(OFFS[o],2,h1),b+3,at(0,1))
    return [s0,s1,s2,s3,s4,s5,s6]

A2A_SEMS=13
def exchange_steps(me,w,src,relay,land,n,base):
    h0=pl.ds(0,n//2); h1=pl.ds(n//2,n//2)
    x1=me.colid(1,me.core); xm=me.colid(-1,me.core)
    def e0():
        for k in range(2):
            far=src(me.colid(2,k))
            w.send(far.at[h0],relay.at[0,k],base+k,base+k,{"col":x1})
            w.send(far.at[h1],relay.at[1,k],base+2+k,base+2+k,{"col":xm})
        for k in range(2):
            w.send(src(me.colid(1,k)),land.at[me.col],base+4+k,base+4+me.core,{"col":me.colid(1,k)})
            w.send(src(me.colid(-1,k)),land.at[me.col],base+6+k,base+6+me.core,{"col":me.colid(-1,k)})
        w.send(src(me.colid(0,1-me.core)),land.at[me.col],base+8,base+8,{"col":me.colid(0,1-me.core)})
    def e1():
        for k in range(2):
            w.got(relay.at[0,k],base+k,{"col":xm})
            w.send(relay.at[0,k],land.at[xm,h0],base+9+k,base+9+me.core,{"col":me.colid(1,k)})
            w.got(relay.at[1,k],base+2+k,{"col":x1})
            w.send(relay.at[1,k],land.at[x1,h1],base+11+k,base+11+me.core,{"col":me.colid(-1,k)})
    def e2():
        for k in range(2):
            w.got(land.at[me.colid(-1,k)],base+4+k,{"col":me.colid(-1,k)})
            w.got(land.at[me.colid(1,k)],base+6+k,{"col":me.colid(1,k)})
        w.got(land.at[me.colid(0,1-me.core)],base+8,{"col":me.colid(0,1-me.core)})
        for k in range(2):
            w.got(land.at[me.colid(2,k),h0],base+9+k,{"col":me.colid(-1,k)})
            w.got(land.at[me.colid(2,k),h1],base+11+k,{"col":me.colid(1,k)})
    return [e0,e1,e2]

RS_SEMS=20
def reduce_steps(me,w,buf,t1,t2,c,c0,t3,t4,lo,n,first,base):
    full=pl.ds(lo,n); h0=pl.ds(lo,n//2); h1=pl.ds(lo+n//2,n//2); g0=pl.ds(0,n//2); g1=pl.ds(n//2,n//2)
    def at(da,db): return {"row":me.rowid(first,da,db)}
    def piece(da,db,rows): return buf.at[me.rowid(first,da,db),rows]
    order=(3,1,2,0)
    def add(ref,other):
        ref[...]=(ref[...].astype(F32)+other[...].astype(F32)).astype(BF)
    def r0():
        for o in order:
            b=base+o*4
            w.send(piece(2,OFFS[o],h0),t1.at[o,0],b,b,at(1,0))
            w.send(piece(2,OFFS[o],h1),t1.at[o,1],b+1,b+1,at(-1,0))
    def r1():
        for o in order:
            b=base+o*4
            w.got(t1.at[o,0],b,at(-1,0)); add(piece(1,OFFS[o],h0),t1.at[o,0])
            w.got(t1.at[o,1],b+1,at(1,0)); add(piece(-1,OFFS[o],h1),t1.at[o,1])
            w.send(piece(1,OFFS[o],full),t2.at[o,0],b+2,b+2,at(1,0))
            w.send(piece(-1,OFFS[o],full),t2.at[o,1],b+3,b+3,at(-1,0))
    def r2():
        for o in order:
            b=base+o*4
            w.got(t2.at[o,0],b+2,at(-1,0)); w.got(t2.at[o,1],b+3,at(1,0))
            total=piece(0,OFFS[o],full)[...].astype(F32)+t2[o,0].astype(F32)+t2[o,1].astype(F32)
            if o==0: c0[...]=total
            else: c[o]=total.astype(BF)
            if o==3:
                w.send(c.at[3,g0],t3.at[0],base+16,base+16,at(0,1))
                w.send(c.at[3,g1],t3.at[1],base+17,base+17,at(0,-1))
    def r3():
        w.got(t3.at[0],base+16,at(0,-1)); add(c.at[2,g0],t3.at[0])
        w.got(t3.at[1],base+17,at(0,1)); add(c.at[1,g1],t3.at[1])
        w.send(c.at[2],t4.at[0],base+18,base+18,at(0,1))
        w.send(c.at[1],t4.at[1],base+19,base+19,at(0,-1))
    def r4():
        w.got(t4.at[0],base+18,at(0,-1)); w.got(t4.at[1],base+19,at(0,1))
        c0[...]+=t4[0].astype(F32)+t4[1].astype(F32)
    return [r0,r1,r2,r3,r4]

def interleave(lists,lag):
    out=[]
    span=max(k*lag+len(l) for k,l in enumerate(lists))
    for t in range(span):
        for k,l in enumerate(lists):
            s=t-k*lag
            if 0<=s<len(l): out.append(l[s])
    return out

def fan_kernel(want_ref,k_ref,v_ref,kv_out,want_out,*scr):
    g=scr[0:4]; s=scr[4:8]; land=scr[8:12]; relay=scr[12]; wv,wsm,ssem,rsem,lsem=scr[13:]
    me=Place(); w=Wires(ssem,rsem)
    me.barrier()
    lb=4*(2*AG_SEMS+A2A_SEMS)
    for d in range(1,8):
        w.send(want_ref,wv.at[me.col],lb+d,lb+d,{"col":(me.col+d)%8})
    def src(q,lo,n):
        ref=(k_ref,v_ref)[q%2]
        return ref.at[pl.ds(lo,n),pl.ds((q//2)*128,128)]
    def lists():
        for d in range(1,8):
            w.got(wv.at[(me.col-d+8)%8],lb+d,{"col":(me.col-d+8)%8})
        a=pltpu.make_async_copy(wv,wsm,lsem.at[0]); a.start(); a.wait()
        b=pltpu.make_async_copy(want_ref,wsm.at[me.col],lsem.at[1]); b.start(); b.wait()
        want_out[...]=wv[...]
        want_out[me.col]=want_ref[...]
    todo=[]
    for q in range(4):
        base=q*(2*AG_SEMS+A2A_SEMS)
        A=gather_steps(me,w,src(q,0,256),g[q],0,256,"z",base)
        B=gather_steps(me,w,src(q,256,256),g[q],256,256,"y",base+AG_SEMS)
        both=[(lambda a=a,b=b:(a(),b())) for a,b in zip(A,B)]
        ex=exchange_steps(me,w,lambda c,q=q:s[q].at[c],relay.at[q],land[q],512,base+2*AG_SEMS)
        def pick(q=q):
            if q==0: lists()
            g[q][me.row]=src(q,0,512)[...]
            for c in range(8):
                rc=wsm[c,0,me.col]
                s[q][c]=g[q][rc]
            land[q][me.col]=s[q][me.col]
        def put(q=q):
            pltpu.make_async_copy(land[q],kv_out.at[q],lsem.at[2+q]).start()
        todo.append(both+[pick]+ex+[put])
    for f in interleave(todo,3): f()
    for q in range(4): pltpu.make_async_copy(land[q],kv_out.at[q],lsem.at[2+q]).wait()
    w.drain()

def fan_out(want,keys,values):
    n=4*(2*AG_SEMS+A2A_SEMS)+8
    return pl.pallas_call(fan_kernel,
        in_specs=[pl.BlockSpec(memory_space=pltpu.VMEM)]*3,
        out_specs=[pl.BlockSpec(memory_space=pl.ANY),pl.BlockSpec(memory_space=pltpu.VMEM)],
        out_shape=[jax.ShapeDtypeStruct((4,8,512,128),BF),jax.ShapeDtypeStruct((8,1,128),jnp.int32)],
        scratch_shapes=[pltpu.VMEM((16,512,128),BF)]*4+[pltpu.VMEM((8,512,128),BF)]*4+[pltpu.VMEM((8,512,128),BF)]*4+[
            pltpu.VMEM((4,2,2,256,128),BF),pltpu.VMEM((8,1,128),jnp.int32),pltpu.SMEM((8,1,128),jnp.int32),
            pltpu.SemaphoreType.DMA((n,)),pltpu.SemaphoreType.DMA((n,)),pltpu.SemaphoreType.DMA((6,))],
        compiler_params=pltpu.CompilerParams(collective_id=0,has_side_effects=True,vmem_limit_bytes=60*2**20),
        name="fan_out")(want,keys,values)

def fan_in_kernel(want_ref,part_ref,dk_ref,dv_ref,*scr):
    a=scr[0:4]; b=scr[4:8]; relay,t1,t2,c,c0,t3,t4,ssem,rsem=scr[8:]
    me=Place(); w=Wires(ssem,rsem)
    me.barrier()
    todo=[]
    for q in range(4):
        base=q*(2*RS_SEMS+A2A_SEMS); gg,kv=q//2,q%2
        ex=exchange_steps(me,w,lambda cc,gg=gg,kv=kv:part_ref.at[cc,gg,kv],relay.at[q],a[q],128,base+2*RS_SEMS)
        def merge(q=q,gg=gg,kv=kv):
            a[q][me.col]=part_ref[me.col,gg,kv]
            rows=[want_ref[cc,0,me.col] for cc in range(8)]
            def block(i,_):
                r=pl.ds(pl.multiple_of((i//2)*16,16),16); l=pl.ds(pl.multiple_of((i%2)*256,256),256)
                vals=[a[q][cc,r,l].astype(F32) for cc in range(8)]
                for R in range(16):
                    t=jnp.where(rows[0]==R,vals[0],0.0)
                    for cc in range(1,8): t=t+jnp.where(rows[cc]==R,vals[cc],0.0)
                    b[q][R,r,l]=t.astype(BF)
                return 0
            lax.fori_loop(0,16,block,0)
        A=reduce_steps(me,w,b[q],t1.at[q,0],t2.at[q,0],c.at[q,0],c0.at[q,0],t3.at[q,0],t4.at[q,0],0,64,"y",base)
        B=reduce_steps(me,w,b[q],t1.at[q,1],t2.at[q,1],c.at[q,1],c0.at[q,1],t3.at[q,1],t4.at[q,1],64,64,"z",base+RS_SEMS)
        both=[(lambda x=x,y=y:(x(),y())) for x,y in zip(A,B)]
        def fin(q=q,gg=gg,kv=kv):
            full=jnp.concatenate([c0[q,0],c0[q,1]],axis=0)
            (dk_ref,dv_ref)[kv][:,gg*128:(gg+1)*128]=full.T.astype(BF)
        todo.append(ex+[merge]+both+[fin])
    for f in interleave(todo,2): f()
    w.drain()

def fan_in(want_all,part):
    n=4*(2*RS_SEMS+A2A_SEMS)
    return pl.pallas_call(fan_in_kernel,
        in_specs=[pl.BlockSpec(memory_space=pltpu.SMEM),pl.BlockSpec(memory_space=pltpu.VMEM)],
        out_specs=[pl.BlockSpec(memory_space=pltpu.VMEM)]*2,
        out_shape=[jax.ShapeDtypeStruct((512,256),BF)]*2,
        scratch_shapes=[pltpu.VMEM((8,128,512),BF)]*4+[pltpu.VMEM((16,128,512),BF)]*4+[
            pltpu.VMEM((4,2,2,64,512),BF),pltpu.VMEM((4,2,4,2,32,512),BF),pltpu.VMEM((4,2,4,2,64,512),BF),
            pltpu.VMEM((4,2,4,64,512),BF),pltpu.VMEM((4,2,64,512),F32),pltpu.VMEM((4,2,2,32,512),BF),pltpu.VMEM((4,2,2,64,512),BF),
            pltpu.SemaphoreType.DMA((n,)),pltpu.SemaphoreType.DMA((n,))],
        compiler_params=pltpu.CompilerParams(collective_id=1,has_side_effects=True,vmem_limit_bytes=60*2**20),
        name="fan_in")(want_all,part)

def wants(table):
    hit=(table%8).reshape(9,1)==jnp.arange(8,dtype=jnp.int32)[None]
    rows=jnp.max(jnp.where(hit,(table//8).reshape(9,1),0),axis=0)
    return jnp.pad(rows,(0,120)).reshape(1,128)
def local(queries,keys,values,output_gradient,tile_block_table):
    me=lax.axis_index("row")*8+lax.axis_index("col")
    info=make_info(tile_block_table,me)
    kv,want_all=fan_out(wants(tile_block_table),keys,values)
    dq,part=attend(queries,output_gradient,kv,info)
    dk,dv=fan_in(want_all,part)
    return dq,dk,dv
def solution(mesh):
    from jax.sharding import PartitionSpec as P
    s=P(("row","col"),None)
    return jax.shard_map(local,mesh=mesh,in_specs=(s,)*5,out_specs=(s,)*3,check_vma=False)
```

time: 984 us -> 262 us (0.27); the launches traced: 970 us -> 262 us
  waiting for transfers between devices: 381 us -> 0 us
  Pallas kernels: 0 us -> 256 us
  matrix products: 194 us -> 0 us
  local copies, waits for them, and re-layouts: 161 us -> 4.71 us
  other arithmetic: 106 us -> 0.91 us
  blocking collectives: 90.5 us -> 0 us
  starting transfers between devices: 23.1 us -> 0 us
  between operations: 14.8 us -> 0.66 us
    all_to_all x4 -> x0, waiting for transfers between devices: 328 us -> none  [the longest x1 283 us: local(): lax.all_to_all(partials.reshape(n_row, cap_row, flat_width), 'row', split...]
    pallas_call x0 -> x3, Pallas kernels: none -> 256 us  [the longest x1 93.5 us: fan_in(): pl.pallas_call(fan_in_kernel, in_specs=[pl.BlockSpec(memory_space=pltpu.S...]
    dot_general x33 -> x0, matrix products: 194 us -> none  [the longest x6 62.7 us: pair_grads(): lax.dot_general(gradient_rows, block_value_rows, forward, preferred_eleme...]
    unnamed x1 -> x0, blocking collectives: 90.5 us -> none
    all_gather x1 -> x0, waiting for transfers between devices: 52.8 us -> none  [local(): lax.all_gather(local_kv, 'row', axis=0, tiled=True)]
    reshape x10 -> x3, local copies, waits for them, and re-layouts: 51.1 us -> 0.68 us  [the longest x1 0.52 us: wants(): return jnp.pad(rows, (0, 120)).reshape(1, 128)]
    convert_element_type x8 -> x0, other arithmetic: 39.9 us -> none  [the longest x6 39.9 us: pair_grads(): (weights * (grad_weights - row_delta) * factor).astype(jnp.bfloat16)]
    while x24 -> x0, local copies, waits for them, and re-layouts: 29.6 us -> none
  transfers between devices with their start and end apart: 5 -> 0, of which waited for: 4 -> 0; matrix products, arithmetic and copies ran while one was open for 5% -> 0% of each run, Pallas kernels for 0% -> 0%
where the time goes in v1:
time: 262 us
  Pallas kernels  256 us (98%)
  local copies, waits for them, and re-layouts  4.71 us (2%)
    pallas_call x1, Pallas kernels, fan_in(): pl.pallas_call(fan_in_kernel, in_specs=[pl.BlockSpec(memory_space=pltpu.S...  93.5 us
    pallas_call x1, Pallas kernels, fan_out(): pl.pallas_call(fan_kernel, in_specs=[pl.BlockSpec(memory_space=pltpu.VMEM...  91.3 us
    pallas_call x1, Pallas kernels, attend(): pl.pallas_call(functools.partial(attn_kernel, hc), grid_spec=pltpu.Prefet...  70.9 us

profile of v1, /device:TPU:0, one launch (start us, length us, event | category | flops | bytes accessed | tf_op | source)
XLA Modules:
  0.0 262.0 jit_solution(16302485640253985783)
XLA Ops:
  0.7 0.7 add_select_fusion
  1.3 0.1 broadcast_in_dim.31
  1.4 0.1 reshape.40
  1.5 0.1 select_reduce_fusion
  1.6 0.1 reshape.44
  1.7 0.6 concatenate.3.info
  2.3 0.1 select_reduce_fusion.1
  2.4 0.5 pad_bitcast_fusion.want_ref
  2.9 91.3 %fan_out.1 = (bf16[4,8,512,128]{3,2,1,0:T(8,128)(2,1)}, s32[8,1,128]{2,1,0:T(1,128)}) custom-call(s32[1,128]{1,0:T(1,128)} %pad_bitcast_fusion.want_ref, bf16[512,256]{1,0:T(8,128)(2,1)} %k_ref.1, bf16[512,256]{1,0:T(8,128)(2,1)} %v_ref.1), custom_call_target="tpu_custom_call" | custom-call | tf_op jit(solution)/shard_map/fan_out/pallas_call | solution.py:270
  94.2 70.9 %attend.1 = (bf16[384,4096]{1,0:T(8,128)(2,1)}, bf16[8,2,2,128,512]{4,3,2,1,0:T(8,128)(2,1)}) custom-call(s32[48]{0:T(128)} %concatenate.3.info, bf16[384,4096]{1,0:T(8,128)(2,1)} %q_ref.1, bf16[384,4096]{1,0:T(8,128)(2,1)} %do_ref.1, bf16[4,8,512,128]{3,2,1,0:T(8,128)(2,1)} %get-tuple-element.9.k_ref.v_ref, ...), custom_call_target="tpu_custom_call" | custom-call | flops 24000000000 | bytes 20000000 | tf_op jit(solution)/shard_map/attend/pallas_call | solution.py:65
  165.1 93.5 %fan_in.1 = (bf16[512,256]{1,0:T(8,128)(2,1)}, bf16[512,256]{1,0:T(8,128)(2,1)}) custom-call(s32[8,1,128]{2,1,0:T(1,128)} %get-tuple-element.11.want_ref, bf16[8,2,2,128,512]{4,3,2,1,0:T(8,128)(2,1)} %get-tuple-element.12.part_ref), custom_call_target="tpu_custom_call" | custom-call | tf_op jit(solution)/shard_map/fan_in/pallas_call | solution.py:312
  258.6 1.7 copy.10
  260.3 1.7 copy.11
  (3 shorter events, 0.0 us)

commit v2 on v1

v2 whole, which is shorter than its diff:
```python
import functools
import jax, jax.numpy as jnp
from jax import lax
from jax.experimental import pallas as pl
from jax.experimental.pallas import tpu as pltpu
NT=(((1,),(1,)),((),()))
NN=(((1,),(0,)),((),()))
BF=jnp.bfloat16; F32=jnp.float32
MESH=pl.DeviceIdType.MESH
OFFS=(0,-1,1,2)

class Place:
    def __init__(self):
        self.row=lax.axis_index("row"); self.col=lax.axis_index("col")
        self.y=self.row//4; self.z=self.row%4; self.x=self.col//2; self.core=self.col%2
    def rowid(self,first,da,db):
        dy,dz=(db,da) if first=="z" else (da,db)
        return ((self.y+dy+4)%4)*4+(self.z+dz+4)%4
    def colid(self,dx,core):
        return ((self.x+dx+4)%4)*2+core
    def barrier(self):
        sem=pltpu.get_barrier_semaphore()
        for d in (1,2,3,4,5,6,7):
            pl.semaphore_signal(sem,inc=1,device_id={"col":(self.col+d)%8},device_id_type=MESH)
        for dy,dz in ((1,0),(-1,0),(0,1),(0,-1)):
            pl.semaphore_signal(sem,inc=1,device_id={"row":((self.y+dy+4)%4)*4+(self.z+dz+4)%4},device_id_type=MESH)
        pl.semaphore_wait(sem,11)

class Wires:
    def __init__(self,ssem,rsem):
        self.ssem=ssem; self.rsem=rsem; self.pending=[]
    def send(self,src,dst,si,ri,where):
        d=pltpu.make_async_remote_copy(src_ref=src,dst_ref=dst,send_sem=self.ssem.at[si],recv_sem=self.rsem.at[ri],device_id=where,device_id_type=MESH)
        d.start(); self.pending.append((src,si))
    def got(self,dst,ri,where):
        pltpu.make_async_remote_copy(src_ref=dst,dst_ref=dst,send_sem=self.ssem.at[0],recv_sem=self.rsem.at[ri],device_id=where,device_id_type=MESH).wait_recv()
    def drain(self):
        for src,si in self.pending:
            root=getattr(src,"ref",src); sh=src.shape
            ref=root.at[(0,)*(len(root.shape)-len(sh))+tuple(pl.ds(0,k) for k in sh)]
            near={"col":(lax.axis_index("col")+1)%8}
            pltpu.make_async_remote_copy(src_ref=ref,dst_ref=ref,send_sem=self.ssem.at[si],recv_sem=self.rsem.at[si],device_id=near,device_id_type=MESH).wait_send()
        self.pending=[]

AG_SEMS=20
def gather_steps(me,w,own,buf,lo,n,first,base):
    full=pl.ds(lo,n); h0=pl.ds(lo,n//2); h1=pl.ds(lo+n//2,n//2)
    def at(da,db): return {"row":me.rowid(first,da,db)}
    def spread(o,src,dst):
        w.send(src,dst,base+4+o*4,base+4+o*4,at(0,1))
        w.send(src,dst,base+5+o*4,base+5+o*4,at(0,-1))
    def piece(da,db,rows): return buf.at[me.rowid(first,da,db),rows]
    def s0():
        w.send(own,piece(0,0,full),base,base,at(1,0))
        w.send(own,piece(0,0,full),base+1,base+1,at(-1,0))
        spread(0,own,piece(0,0,full))
    def s1():
        w.got(piece(-1,0,full),base,at(-1,0))
        w.send(piece(-1,0,h0),piece(-1,0,h0),base+2,base+2,at(1,0))
        spread(1,piece(-1,0,full),piece(-1,0,full))
        w.got(piece(1,0,full),base+1,at(1,0))
        w.send(piece(1,0,h1),piece(1,0,h1),base+3,base+3,at(-1,0))
        spread(2,piece(1,0,full),piece(1,0,full))
    def turn(o):
        da=OFFS[o]; b=base+4+o*4
        w.got(piece(da,-1,full),b,at(0,-1))
        w.send(piece(da,-1,h0),piece(da,-1,h0),b+2,b+2,at(0,1))
        w.got(piece(da,1,full),b+1,at(0,1))
        w.send(piece(da,1,h1),piece(da,1,h1),b+3,b+3,at(0,-1))
    def s2(): turn(0)
    def s3():
        w.got(piece(2,0,h0),base+2,at(-1,0))
        w.got(piece(2,0,h1),base+3,at(1,0))
        spread(3,piece(2,0,full),piece(2,0,full))
    def s4(): turn(1); turn(2)
    def s5(): turn(3)
    def s6():
        for o in range(4):
            b=base+4+o*4
            w.got(piece(OFFS[o],2,h0),b+2,at(0,-1))
            w.got(piece(OFFS[o],2,h1),b+3,at(0,1))
    return [s0,s1,s2,s3,s4,s5,s6]

A2A_SEMS=13
def exchange_steps(me,w,src,relay,land,n,base):
    h0=pl.ds(0,n//2); h1=pl.ds(n//2,n//2)
    x1=me.colid(1,me.core); xm=me.colid(-1,me.core)
    def e0():
        for k in range(2):
            far=src(me.colid(2,k))
            w.send(far.at[h0],relay.at[0,k],base+k,base+k,{"col":x1})
            w.send(far.at[h1],relay.at[1,k],base+2+k,base+2+k,{"col":xm})
        for k in range(2):
            w.send(src(me.colid(1,k)),land.at[me.col],base+4+k,base+4+me.core,{"col":me.colid(1,k)})
            w.send(src(me.colid(-1,k)),land.at[me.col],base+6+k,base+6+me.core,{"col":me.colid(-1,k)})
        w.send(src(me.colid(0,1-me.core)),land.at[me.col],base+8,base+8,{"col":me.colid(0,1-me.core)})
    def e1():
        for k in range(2):
            w.got(relay.at[0,k],base+k,{"col":xm})
            w.send(relay.at[0,k],land.at[xm,h0],base+9+k,base+9+me.core,{"col":me.colid(1,k)})
            w.got(relay.at[1,k],base+2+k,{"col":x1})
            w.send(relay.at[1,k],land.at[x1,h1],base+11+k,base+11+me.core,{"col":me.colid(-1,k)})
    def e2():
        for k in range(2):
            w.got(land.at[me.colid(-1,k)],base+4+k,{"col":me.colid(-1,k)})
            w.got(land.at[me.colid(1,k)],base+6+k,{"col":me.colid(1,k)})
        w.got(land.at[me.colid(0,1-me.core)],base+8,{"col":me.colid(0,1-me.core)})
        for k in range(2):
            w.got(land.at[me.colid(2,k),h0],base+9+k,{"col":me.colid(-1,k)})
            w.got(land.at[me.colid(2,k),h1],base+11+k,{"col":me.colid(1,k)})
    return [e0,e1,e2]

RS_SEMS=20
def reduce_steps(me,w,buf,t1,t2,c,c0,t3,t4,lo,n,first,base):
    full=pl.ds(lo,n); h0=pl.ds(lo,n//2); h1=pl.ds(lo+n//2,n//2); g0=pl.ds(0,n//2); g1=pl.ds(n//2,n//2)
    def at(da,db): return {"row":me.rowid(first,da,db)}
    def piece(da,db,rows): return buf.at[me.rowid(first,da,db),rows]
    order=(3,1,2,0)
    def add(ref,other):
        ref[...]=(ref[...].astype(F32)+other[...].astype(F32)).astype(BF)
    def r0():
        for o in order:
            b=base+o*4
            w.send(piece(2,OFFS[o],h0),t1.at[o,0],b,b,at(1,0))
            w.send(piece(2,OFFS[o],h1),t1.at[o,1],b+1,b+1,at(-1,0))
    def r1():
        for o in order:
            b=base+o*4
            w.got(t1.at[o,0],b,at(-1,0)); add(piece(1,OFFS[o],h0),t1.at[o,0])
            w.got(t1.at[o,1],b+1,at(1,0)); add(piece(-1,OFFS[o],h1),t1.at[o,1])
            w.send(piece(1,OFFS[o],full),t2.at[o,0],b+2,b+2,at(1,0))
            w.send(piece(-1,OFFS[o],full),t2.at[o,1],b+3,b+3,at(-1,0))
    def r2():
        for o in order:
            b=base+o*4
            w.got(t2.at[o,0],b+2,at(-1,0)); w.got(t2.at[o,1],b+3,at(1,0))
            total=piece(0,OFFS[o],full)[...].astype(F32)+t2[o,0].astype(F32)+t2[o,1].astype(F32)
            if o==0: c0[...]=total
            else: c[o]=total.astype(BF)
            if o==3:
                w.send(c.at[3,g0],t3.at[0],base+16,base+16,at(0,1))
                w.send(c.at[3,g1],t3.at[1],base+17,base+17,at(0,-1))
    def r3():
        w.got(t3.at[0],base+16,at(0,-1)); add(c.at[2,g0],t3.at[0])
        w.got(t3.at[1],base+17,at(0,1)); add(c.at[1,g1],t3.at[1])
        w.send(c.at[2],t4.at[0],base+18,base+18,at(0,1))
        w.send(c.at[1],t4.at[1],base+19,base+19,at(0,-1))
    def r4():
        w.got(t4.at[0],base+18,at(0,-1)); w.got(t4.at[1],base+19,at(0,1))
        c0[...]+=t4[0].astype(F32)+t4[1].astype(F32)
    return [r0,r1,r2,r3,r4]

def interleave(lists,lag):
    out=[]
    span=max(k*lag+len(l) for k,l in enumerate(lists))
    for t in range(span):
        for k,l in enumerate(lists):
            s=t-k*lag
            if 0<=s<len(l): out.append(l[s])
    return out

def make_info(table, my_device):
    slots=table%8
    tiles=my_device*3+jnp.arange(3,dtype=jnp.int32)
    hit=slots[:,None,:]==jnp.arange(8,dtype=jnp.int32)[None,:,None]
    ent=jnp.arange(9,dtype=jnp.int32).reshape(3,1,3)
    idx=jnp.min(jnp.where(hit,ent,9),axis=2)
    return jnp.concatenate([slots.reshape(9),jnp.zeros(9,jnp.int32),tiles%4,jnp.zeros(3,jnp.int32),idx.reshape(24)])
HC=2
NCH=16//HC
ITERS=3*NCH
LB=4*(2*AG_SEMS+A2A_SEMS)
IB=LB+8
NSEM=IB+4*(2*RS_SEMS+A2A_SEMS)

def attend_unit(g,it,hc,info,qb,db,kb,vb,acc):
    scale=128**-0.5
    c=scale*1.4426950408889634
    rows=hc*128
    tile=it//NCH
    off=pl.multiple_of(g*2048+(it%NCH)*rows,rows)
    rsl=pl.ds(pl.multiple_of(tile*128,128),128)
    diag=info[18+tile]*128
    slots=[info[tile*3+j] for j in range(3)]
    q2=qb[rsl,pl.ds(off,rows)]; d2=db[rsl,pl.ds(off,rows)]
    q=jnp.concatenate([q2[:,h*128:(h+1)*128] for h in range(hc)],axis=0)
    d=jnp.concatenate([d2[:,h*128:(h+1)*128] for h in range(hc)],axis=0)
    ks=[kb[slots[j]] for j in range(3)]
    vs=[vb[slots[j]] for j in range(3)]
    s=[lax.dot_general(q,ks[j],NT,preferred_element_type=F32) for j in range(3)]
    r=lax.broadcasted_iota(jnp.int32,(rows,512),0)&127
    col=lax.broadcasted_iota(jnp.int32,(rows,512),1)
    s[0]=jnp.where(col<=r+diag,s[0],-jnp.inf)
    m=jnp.max(jnp.maximum(jnp.maximum(s[0],s[1]),s[2]),axis=1,keepdims=True)*c
    p=[jnp.exp2(x*c-m) for x in s]
    l=jnp.sum(p[0]+p[1]+p[2],axis=1,keepdims=True)
    dp=[lax.dot_general(d,vs[j],NT,preferred_element_type=F32) for j in range(3)]
    t=jnp.sum(p[0]*dp[0]+p[1]*dp[1]+p[2]*dp[2],axis=1,keepdims=True)
    inv=1.0/l
    delta=t*inv
    p=[p[j]*inv for j in range(3)]
    ds=[(p[j]*(dp[j]-delta)*scale).astype(BF) for j in range(3)]
    pb=[p[j].astype(BF) for j in range(3)]
    dq=sum(lax.dot_general(ds[j],ks[j],NN,preferred_element_type=F32) for j in range(3)).astype(BF)
    for h in range(hc):
        qb[rsl,pl.ds(off+h*128,128)]=dq[h*128:(h+1)*128]
    qT=q.T
    dT=d.T
    for j in range(3):
        acc[tile*3+j,0]+=lax.dot_general(qT,ds[j],NN,preferred_element_type=F32)
        acc[tile*3+j,1]+=lax.dot_general(dT,pb[j],NN,preferred_element_type=F32)

def mega_kernel(info,want_ref,k_ref,v_ref,q_hbm,do_hbm,dq_hbm,dk_ref,dv_ref,*scr):
    scr=list(scr)
    take=lambda n:[scr.pop(0) for _ in range(n)]
    gat=take(4); pickd=take(2); land=take(4); relay1,wv,wsm=take(3)
    qb,db,acc=take(3); part=take(2); back=take(4); sums=take(2)
    relay2,t1,t2,c,c0,t3,t4=take(7); ssem,rsem,lsem=take(3)
    me=Place(); w=Wires(ssem,rsem)
    qc=pltpu.make_async_copy(q_hbm,qb,lsem.at[2]); qc.start()
    dc=pltpu.make_async_copy(do_hbm,db,lsem.at[3]); dc.start()
    me.barrier()
    for d in range(1,8):
        w.send(want_ref,wv.at[me.col],LB+d,LB+d,{"col":(me.col+d)%8})
    def src(q,lo,n):
        return (k_ref,v_ref)[q%2].at[pl.ds(lo,n),pl.ds((q//2)*128,128)]
    def lists():
        for d in range(1,8):
            w.got(wv.at[(me.col-d+8)%8],LB+d,{"col":(me.col-d+8)%8})
        a=pltpu.make_async_copy(wv,wsm,lsem.at[0]); a.start(); a.wait()
        b=pltpu.make_async_copy(want_ref,wsm.at[me.col],lsem.at[1]); b.start(); b.wait()
    exw=[Wires(ssem,rsem) for _ in range(4)]
    out=[]
    for q in range(4):
        base=q*(2*AG_SEMS+A2A_SEMS)
        A=gather_steps(me,w,src(q,0,256),gat[q],0,256,"z",base)
        B=gather_steps(me,w,src(q,256,256),gat[q],256,256,"y",base+AG_SEMS)
        both=[(lambda a=a,b=b:(a(),b())) for a,b in zip(A,B)]
        ex=exchange_steps(me,exw[q],lambda cc,q=q:pickd[q%2].at[cc],relay1.at[q],land[q],512,base+2*AG_SEMS)
        def pick(q=q):
            if q==0: lists()
            if q>=2: exw[q-2].drain()
            gat[q][me.row]=src(q,0,512)[...]
            for cc in range(8):
                pickd[q%2][cc]=gat[q][wsm[cc,0,me.col]]
            land[q][me.col]=pickd[q%2][me.col]
        out.append(both+[pick]+ex)
    n=len(out[0])
    redw=[Wires(ssem,rsem) for _ in range(4)]
    ret=[]
    for q in range(4):
        base=IB+q*(2*RS_SEMS+A2A_SEMS); gg,kv=q//2,q%2
        ex=exchange_steps(me,w,lambda cc,gg=gg,kv=kv:part[gg].at[cc,kv],relay2.at[q],back[q],128,base+2*RS_SEMS)
        def merge(q=q,gg=gg,kv=kv):
            if q>=2: redw[q-2].drain()
            a=back[q]; b=sums[q%2]
            a[me.col]=part[gg][me.col,kv]
            rows=[wsm[cc,0,me.col] for cc in range(8)]
            def block(i,_):
                r=pl.ds(pl.multiple_of((i//2)*16,16),16); ln=pl.ds(pl.multiple_of((i%2)*256,256),256)
                vals=[a[cc,r,ln].astype(F32) for cc in range(8)]
                for R in range(16):
                    t=jnp.where(rows[0]==R,vals[0],0.0)
                    for cc in range(1,8): t=t+jnp.where(rows[cc]==R,vals[cc],0.0)
                    b[R,r,ln]=t.astype(BF)
                return 0
            lax.fori_loop(0,16,block,0)
        A=reduce_steps(me,redw[q],sums[q%2],t1.at[q,0],t2.at[q,0],c.at[q,0],c0.at[0],t3.at[q,0],t4.at[q,0],0,64,"y",base)
        B=reduce_steps(me,redw[q],sums[q%2],t1.at[q,1],t2.at[q,1],c.at[q,1],c0.at[1],t3.at[q,1],t4.at[q,1],64,64,"z",base+RS_SEMS)
        both=[(lambda x=x,y=y:(x(),y())) for x,y in zip(A,B)]
        def fin(q=q,gg=gg,kv=kv):
            (dk_ref,dv_ref)[kv][:,gg*128:(gg+1)*128]=jnp.concatenate([c0[0],c0[1]],axis=0).T.astype(BF)
        ret.append(ex+[merge]+both[:-1]+[lambda last=both[-1],fin=fin:(last(),fin())])
    def zero():
        acc[...]=jnp.zeros_like(acc)
    def compute(g,hooks):
        def one(it,_):
            for k in sorted(hooks):
                @pl.when(it==k)
                def _(k=k):
                    for f in hooks[k]: f()
            attend_unit(g,it,HC,info,qb,db,land[2*g],land[2*g+1],acc)
            return 0
        lax.fori_loop(0,ITERS,one,0)
        for sl in range(8):
            for kv in range(2):
                part[g][sl,kv]=(acc[info[24+sl],kv]+acc[info[32+sl],kv]+acc[info[40+sl],kv]).astype(BF)
        cp=pltpu.make_async_copy(qb.at[:,pl.ds(g*2048,2048)],dq_hbm.at[:,pl.ds(g*2048,2048)],lsem.at[4+g])
        cp.start()
        return cp
    LAG=3
    first=LAG+n
    def at(t): return [out[k][t-k*LAG] for k in range(4) if 0<=t-k*LAG<n]
    for t in range(first):
        for f in at(t): f()
        if t==4: zero()
    qc.wait(); dc.wait()
    later=[at(t) for t in range(first,3*LAG+n)]
    hooks0={OUT_IT[i]:fs for i,fs in enumerate(later)}
    cp0=compute(0,hooks0)
    zero()
    hooks1={}
    for q,its in enumerate((RET0,RET1)):
        for f,i in zip(ret[q],its): hooks1.setdefault(i,[]).append(f)
    cp1=compute(1,hooks1)
    for f in interleave(ret[2:],2): f()
    cp0.wait(); cp1.wait()
    w.drain()
    for x in exw[2:]+redw[2:]: x.drain()

OUT_IT=(2,6,10,14,18,22)
RET0=(0,4,9,9,9,12,14,16,18)
RET1=(4,10,15,15,15,18,20,22,23)

def mega(info,want,queries,keys,values,output_gradient):
    V=lambda *sh,dt=BF: pltpu.VMEM(sh,dt)
    vm=pl.BlockSpec(memory_space=pltpu.VMEM); anyspec=pl.BlockSpec(memory_space=pl.ANY)
    return pl.pallas_call(mega_kernel,
        in_specs=[pl.BlockSpec(memory_space=pltpu.SMEM),vm,vm,vm,anyspec,anyspec],
        out_specs=[anyspec,vm,vm],
        out_shape=[jax.ShapeDtypeStruct((384,4096),BF)]+[jax.ShapeDtypeStruct((512,256),BF)]*2,
        scratch_shapes=[V(16,512,128)]*4+[V(8,512,128)]*2+[V(8,512,128)]*4+[V(4,2,2,256,128),V(8,1,128,dt=jnp.int32),pltpu.SMEM((8,1,128),jnp.int32)]
            +[V(384,4096),V(384,4096),V(10,2,128,512,dt=F32)]+[V(8,2,128,512)]*2+[V(8,128,512)]*4+[V(16,128,512)]*2
            +[V(4,2,2,64,512),V(4,2,4,2,32,512),V(4,2,4,2,64,512),V(4,2,4,64,512),V(2,64,512,dt=F32),V(4,2,2,32,512),V(4,2,2,64,512)]
            +[pltpu.SemaphoreType.DMA((NSEM,)),pltpu.SemaphoreType.DMA((NSEM,)),pltpu.SemaphoreType.DMA((6,))],
        compiler_params=pltpu.CompilerParams(collective_id=0,has_side_effects=True,vmem_limit_bytes=67043328),
        name="mega")(info,want,keys,values,queries,output_gradient)
def wants(table):
    hit=(table%8).reshape(9,1)==jnp.arange(8,dtype=jnp.int32)[None]
    rows=jnp.max(jnp.where(hit,(table//8).reshape(9,1),0),axis=0)
    return jnp.pad(rows,(0,120)).reshape(1,128)
def local(queries,keys,values,output_gradient,tile_block_table):
    me=lax.axis_index("row")*8+lax.axis_index("col")
    info=make_info(tile_block_table,me)
    return mega(info,wants(tile_block_table),queries,keys,values,output_gradient)
def solution(mesh):
    from jax.sharding import PartitionSpec as P
    s=P(("row","col"),None)
    return jax.shard_map(local,mesh=mesh,in_specs=(s,)*5,out_specs=(s,)*3,check_vma=False)
```

time: 262 us -> 230 us (0.88)
  Pallas kernels: 256 us -> 221 us
    pallas_call x3 -> x1, Pallas kernels: 256 us -> 221 us  [mega(): pl.pallas_call(mega_kernel, in_specs=[pl.BlockSpec(memory_space=pltpu.SME...]
    unnamed x2 -> x7, local copies, waits for them, and re-layouts: 3.34 us -> 5.38 us
where the time goes in v2:
time: 230 us; the launch traced here: 229 us
  Pallas kernels  221 us (96%)
  local copies, waits for them, and re-layouts  6.75 us (3%)
    pallas_call x1, Pallas kernels, mega(): pl.pallas_call(mega_kernel, in_specs=[pl.BlockSpec(memory_space=pltpu.SME...  221 us
    unnamed x7, local copies, waits for them, and re-layouts  5.38 us

profile of v2, /device:TPU:0, one launch (start us, length us, event | category | flops | bytes accessed | tf_op | source)
XLA Modules:
  0.0 229.3 jit_solution(10733624164569010579)
XLA Ops:
  0.7 0.7 add_select_fusion
  1.3 0.1 broadcast_in_dim.31
  1.4 0.1 reshape.40
  1.5 0.1 select_reduce_fusion
  1.6 0.1 reshape.44
  1.7 0.6 concatenate.3.info
  2.3 0.1 select_reduce_fusion.1
  2.4 0.5 pad_bitcast_fusion.want_ref
  2.9 221.0 %mega.1 = (bf16[384,4096]{1,0:T(8,128)(2,1)}, bf16[512,256]{1,0:T(8,128)(2,1)}, bf16[512,256]{1,0:T(8,128)(2,1)}) custom-call(s32[48]{0:T(128)} %concatenate.3.info, s32[1,128]{1,0:T(1,128)} %pad_bitcast_fusion.want_ref, bf16[512,256]{1,0:T(8,128)(2,1)} %k_ref.1, bf16[512,256]{1,0:T(8,128)(2,1)} %v_ref.1, bf16[384,4096]{1,0:T(8,128)(2,1)} %q_hbm.1, ...), custom_call_target="tpu_custom_call" | custom-call | tf_op jit(solution)/shard_map/mega/pallas_call | solution.py:318
  223.9 0.0 copy-start.1
  223.9 0.0 copy-start
  223.9 4.0 %copy.11 = bf16[384,4096]{1,0:T(8,128)(2,1)} copy(bf16[384,4096]{1,0:T(8,128)(2,1)} %get-tuple-element.9) | data formatting | bytes 6291456
  227.9 0.0 copy-done.1
  227.9 0.7 copy.12
  228.6 0.0 copy-done
  228.6 0.7 copy.13
  (3 shorter events, 0.0 us)
Async XLA Ops:
  223.9 4.0 %copy-start.1 = (bf16[512,256]{1,0:T(8,128)(2,1)S(1)}, bf16[512,256]{1,0:T(8,128)(2,1)}, u32[]{:S(2)}) copy-start(bf16[512,256]{1,0:T(8,128)(2,1)} %get-tuple-element.10) | copy-start | bytes 786436
  223.9 4.7 %copy-start = (bf16[512,256]{1,0:T(8,128)(2,1)S(1)}, bf16[512,256]{1,0:T(8,128)(2,1)}, u32[]{:S(2)}) copy-start(bf16[512,256]{1,0:T(8,128)(2,1)} %get-tuple-element.11) | copy-start | bytes 786436

commit v3 on v2

--- a/solution.py
+++ b/solution.py
@@ -159,66 +159,84 @@
             if 0<=s<len(l): out.append(l[s])
     return out
 
-def make_info(table, my_device):
-    slots=table%8
-    tiles=my_device*3+jnp.arange(3,dtype=jnp.int32)
-    hit=slots[:,None,:]==jnp.arange(8,dtype=jnp.int32)[None,:,None]
-    ent=jnp.arange(9,dtype=jnp.int32).reshape(3,1,3)
-    idx=jnp.min(jnp.where(hit,ent,9),axis=2)
-    return jnp.concatenate([slots.reshape(9),jnp.zeros(9,jnp.int32),tiles%4,jnp.zeros(3,jnp.int32),idx.reshape(24)])
 HC=2
 NCH=16//HC
-ITERS=3*NCH
+ITERS=3*NCH//2
 LB=4*(2*AG_SEMS+A2A_SEMS)
 IB=LB+8
 NSEM=IB+4*(2*RS_SEMS+A2A_SEMS)
 
-def attend_unit(g,it,hc,info,qb,db,kb,vb,acc):
+def attend_pair(g,it,hc,info,qb,db,kb,vb,acc):
     scale=128**-0.5
     c=scale*1.4426950408889634
     rows=hc*128
-    tile=it//NCH
-    off=pl.multiple_of(g*2048+(it%NCH)*rows,rows)
+    tile=it//(NCH//2)
     rsl=pl.ds(pl.multiple_of(tile*128,128),128)
     diag=info[18+tile]*128
     slots=[info[tile*3+j] for j in range(3)]
-    q2=qb[rsl,pl.ds(off,rows)]; d2=db[rsl,pl.ds(off,rows)]
-    q=jnp.concatenate([q2[:,h*128:(h+1)*128] for h in range(hc)],axis=0)
-    d=jnp.concatenate([d2[:,h*128:(h+1)*128] for h in range(hc)],axis=0)
-    ks=[kb[slots[j]] for j in range(3)]
-    vs=[vb[slots[j]] for j in range(3)]
-    s=[lax.dot_general(q,ks[j],NT,preferred_element_type=F32) for j in range(3)]
-    r=lax.broadcasted_iota(jnp.int32,(rows,512),0)&127
-    col=lax.broadcasted_iota(jnp.int32,(rows,512),1)
-    s[0]=jnp.where(col<=r+diag,s[0],-jnp.inf)
-    m=jnp.max(jnp.maximum(jnp.maximum(s[0],s[1]),s[2]),axis=1,keepdims=True)*c
-    p=[jnp.exp2(x*c-m) for x in s]
-    l=jnp.sum(p[0]+p[1]+p[2],axis=1,keepdims=True)
-    dp=[lax.dot_general(d,vs[j],NT,preferred_element_type=F32) for j in range(3)]
-    t=jnp.sum(p[0]*dp[0]+p[1]*dp[1]+p[2]*dp[2],axis=1,keepdims=True)
-    inv=1.0/l
-    delta=t*inv
-    p=[p[j]*inv for j in range(3)]
-    ds=[(p[j]*(dp[j]-delta)*scale).astype(BF) for j in range(3)]
-    pb=[p[j].astype(BF) for j in range(3)]
-    dq=sum(lax.dot_general(ds[j],ks[j],NN,preferred_element_type=F32) for j in range(3)).astype(BF)
-    for h in range(hc):
-        qb[rsl,pl.ds(off+h*128,128)]=dq[h*128:(h+1)*128]
-    qT=q.T
-    dT=d.T
-    for j in range(3):
-        acc[tile*3+j,0]+=lax.dot_general(qT,ds[j],NN,preferred_element_type=F32)
-        acc[tile*3+j,1]+=lax.dot_general(dT,pb[j],NN,preferred_element_type=F32)
-
-def mega_kernel(info,want_ref,k_ref,v_ref,q_hbm,do_hbm,dq_hbm,dk_ref,dv_ref,*scr):
+    def load(u):
+        off=pl.multiple_of(g*2048+((it%(NCH//2))*2+u)*rows,rows)
+        q2=qb[rsl,pl.ds(off,rows)]; d2=db[rsl,pl.ds(off,rows)]
+        q=jnp.concatenate([q2[:,h*128:(h+1)*128] for h in range(hc)],axis=0)
+        d=jnp.concatenate([d2[:,h*128:(h+1)*128] for h in range(hc)],axis=0)
+        return off,q,d
+    def products(x):
+        _,q,d=x
+        s=[lax.dot_general(q,kb[slots[j]],NT,preferred_element_type=F32) for j in range(3)]
+        dp=[lax.dot_general(d,vb[slots[j]],NT,preferred_element_type=F32) for j in range(3)]
+        return s,dp
+    def soft(s,dp):
+        r=lax.broadcasted_iota(jnp.int32,(rows,512),0)&127
+        col=lax.broadcasted_iota(jnp.int32,(rows,512),1)
+        s=[jnp.where(col<=r+diag,s[0],-jnp.inf),s[1],s[2]]
+        m=jnp.max(jnp.maximum(jnp.maximum(s[0],s[1]),s[2]),axis=1,keepdims=True)*c
+        p=[jnp.exp2(x*c-m) for x in s]
+        l=jnp.sum(p[0]+p[1]+p[2],axis=1,keepdims=True)
+        t=jnp.sum(p[0]*dp[0]+p[1]*dp[1]+p[2]*dp[2],axis=1,keepdims=True)
+        inv=1.0/l
+        delta=t*inv
+        p=[x*inv for x in p]
+        return [(p[j]*(dp[j]-delta)*scale).astype(BF) for j in range(3)],[x.astype(BF) for x in p]
+    def grads(x,ds,pb):
+        off,q,d=x
+        dq=sum(lax.dot_general(ds[j],kb[slots[j]],NN,preferred_element_type=F32) for j in range(3)).astype(BF)
+        for h in range(hc):
+            qb[rsl,pl.ds(off+h*128,128)]=dq[h*128:(h+1)*128]
+        qT=q.T
+        dT=d.T
+        for j in range(3):
+            acc[tile*3+j,0]+=lax.dot_general(qT,ds[j],NN,preferred_element_type=F32)
+            acc[tile*3+j,1]+=lax.dot_general(dT,pb[j],NN,preferred_element_type=F32)
+    x0=load(0); w0=soft(*products(x0))
+    x1=load(1); n1=products(x1)
+    grads(x0,*w0)
+    grads(x1,*soft(*n1))
+
+def mega_kernel(table_ref,k_ref,v_ref,q_hbm,do_hbm,dq_hbm,dk_ref,dv_ref,*scr):
     scr=list(scr)
     take=lambda n:[scr.pop(0) for _ in range(n)]
     gat=take(4); pickd=take(2); land=take(4); relay1,wv,wsm=take(3)
     qb,db,acc=take(3); part=take(2); back=take(4); sums=take(2)
-    relay2,t1,t2,c,c0,t3,t4=take(7); ssem,rsem,lsem=take(3)
+    relay2,t1,t2,c,c0,t3,t4=take(7); ssem,rsem,lsem,info,want_ref=take(5)
     me=Place(); w=Wires(ssem,rsem)
     qc=pltpu.make_async_copy(q_hbm,qb,lsem.at[2]); qc.start()
     dc=pltpu.make_async_copy(do_hbm,db,lsem.at[3]); dc.start()
+    ids=[[table_ref[i,j] for j in range(3)] for i in range(3)]
+    for i in range(3):
+        for j in range(3): info[i*3+j]=ids[i][j]&7
+        info[18+i]=((me.row*8+me.col)*3+i)%4
+        for sl in range(8):
+            e=jnp.int32(9)
+            for j in range(3): e=jnp.where((ids[i][j]&7)==sl,i*3+j,e)
+            info[24+i*8+sl]=e
+    lane=lax.broadcasted_iota(jnp.int32,(1,128),1)
+    mine=jnp.zeros((1,128),jnp.int32)
+    for sl in range(8):
+        e=jnp.int32(0)
+        for i in range(3):
+            for j in range(3): e=jnp.where((ids[i][j]&7)==sl,ids[i][j]//8,e)
+        mine=jnp.where(lane==sl,e,mine)
+    want_ref[...]=mine
     me.barrier()
     for d in range(1,8):
         w.send(want_ref,wv.at[me.col],LB+d,LB+d,{"col":(me.col+d)%8})
@@ -245,7 +263,6 @@
                 pickd[q%2][cc]=gat[q][wsm[cc,0,me.col]]
             land[q][me.col]=pickd[q%2][me.col]
         out.append(both+[pick]+ex)
-    n=len(out[0])
     redw=[Wires(ssem,rsem) for _ in range(4)]
     ret=[]
     for q in range(4):
@@ -256,20 +273,21 @@
             a=back[q]; b=sums[q%2]
             a[me.col]=part[gg][me.col,kv]
             rows=[wsm[cc,0,me.col] for cc in range(8)]
+            nothing=jnp.zeros((16,256),BF)
             def block(i,_):
                 r=pl.ds(pl.multiple_of((i//2)*16,16),16); ln=pl.ds(pl.multiple_of((i%2)*256,256),256)
-                vals=[a[cc,r,ln].astype(F32) for cc in range(8)]
+                vals=[a[cc,r,ln] for cc in range(8)]
                 for R in range(16):
-                    t=jnp.where(rows[0]==R,vals[0],0.0)
-                    for cc in range(1,8): t=t+jnp.where(rows[cc]==R,vals[cc],0.0)
-                    b[R,r,ln]=t.astype(BF)
+                    t=[jnp.where(rows[cc]==R,vals[cc],nothing) for cc in range(8)]
+                    while len(t)>1: t=[t[k]+t[k+1] for k in range(0,len(t),2)]
+                    b[R,r,ln]=t[0]
                 return 0
             lax.fori_loop(0,16,block,0)
-        A=reduce_steps(me,redw[q],sums[q%2],t1.at[q,0],t2.at[q,0],c.at[q,0],c0.at[0],t3.at[q,0],t4.at[q,0],0,64,"y",base)
-        B=reduce_steps(me,redw[q],sums[q%2],t1.at[q,1],t2.at[q,1],c.at[q,1],c0.at[1],t3.at[q,1],t4.at[q,1],64,64,"z",base+RS_SEMS)
+        A=reduce_steps(me,redw[q],sums[q%2],t1.at[q,0],t2.at[q,0],c.at[q,0],c0.at[q,0],t3.at[q,0],t4.at[q,0],0,64,"y",base)
+        B=reduce_steps(me,redw[q],sums[q%2],t1.at[q,1],t2.at[q,1],c.at[q,1],c0.at[q,1],t3.at[q,1],t4.at[q,1],64,64,"z",base+RS_SEMS)
         both=[(lambda x=x,y=y:(x(),y())) for x,y in zip(A,B)]
         def fin(q=q,gg=gg,kv=kv):
-            (dk_ref,dv_ref)[kv][:,gg*128:(gg+1)*128]=jnp.concatenate([c0[0],c0[1]],axis=0).T.astype(BF)
+            (dk_ref,dv_ref)[kv][:,gg*128:(gg+1)*128]=jnp.concatenate([c0[q,0],c0[q,1]],axis=0).T.astype(BF)
         ret.append(ex+[merge]+both[:-1]+[lambda last=both[-1],fin=fin:(last(),fin())])
     def zero():
         acc[...]=jnp.zeros_like(acc)
@@ -279,7 +297,7 @@
                 @pl.when(it==k)
                 def _(k=k):
                     for f in hooks[k]: f()
-            attend_unit(g,it,HC,info,qb,db,land[2*g],land[2*g+1],acc)
+            attend_pair(g,it,HC,info,qb,db,land[2*g],land[2*g+1],acc)
             return 0
         lax.fori_loop(0,ITERS,one,0)
         for sl in range(8):
@@ -288,51 +306,55 @@
         cp=pltpu.make_async_copy(qb.at[:,pl.ds(g*2048,2048)],dq_hbm.at[:,pl.ds(g*2048,2048)],lsem.at[4+g])
         cp.start()
         return cp
-    LAG=3
-    first=LAG+n
-    def at(t): return [out[k][t-k*LAG] for k in range(4) if 0<=t-k*LAG<n]
-    for t in range(first):
-        for f in at(t): f()
-        if t==4: zero()
+    names=("s0","s1","s2","s3","s4","s5","s6","pick","e0","e1","e2")
+    go={f"{nm}{q}":out[q][i] for q in range(4) for i,nm in enumerate(names)}
+    names=("x0","x1","x2","merge","r0","r1","r2","r3","r4")
+    go.update({f"{nm}{q}":ret[q][i] for q in range(4) for i,nm in enumerate(names)})
+    done=[]
+    def run(text):
+        for nm in text.split(): done.append(nm); go[nm]()
+    def hooks_of(table):
+        return {it:[lambda text=text: run(text)] for it,text in table}
+    for text in BEFORE:
+        run(text)
+        if text==ZERO_AFTER: zero()
     qc.wait(); dc.wait()
-    later=[at(t) for t in range(first,3*LAG+n)]
-    hooks0={OUT_IT[i]:fs for i,fs in enumerate(later)}
-    cp0=compute(0,hooks0)
+    cp0=compute(0,hooks_of(UNDER0))
     zero()
-    hooks1={}
-    for q,its in enumerate((RET0,RET1)):
-        for f,i in zip(ret[q],its): hooks1.setdefault(i,[]).append(f)
-    cp1=compute(1,hooks1)
-    for f in interleave(ret[2:],2): f()
+    cp1=compute(1,hooks_of(UNDER1))
+    for text in AFTER: run(text)
+    assert len(done)==len(go) and len(set(done))==len(done)
     cp0.wait(); cp1.wait()
     w.drain()
     for x in exw[2:]+redw[2:]: x.drain()
 
-OUT_IT=(2,6,10,14,18,22)
-RET0=(0,4,9,9,9,12,14,16,18)
-RET1=(4,10,15,15,15,18,20,22,23)
-
-def mega(info,want,queries,keys,values,output_gradient):
+def stagger(offsets,count,names):
+    rows=[]
+    for t in range(count):
+        rows.append(" ".join(f"{nm}{k}" for k,o in enumerate(offsets) for i,nm in enumerate(names) if i==t-o))
+    return rows
+STEPS=("s0","s1","s2","s3","s4","s5","s6","pick","e0","e1","e2")
+BEFORE=stagger((0,1,5,6),11,STEPS)+["e21"]
+ZERO_AFTER=BEFORE[4]
+UNDER0=((0,"s62 pick2 e02"),(1,"s53"),(2,"s63 pick3 e12 e03"),(5,"e13"),(11,"e22 e23"))
+UNDER1=((0,"x00"),(2,"x10 x01"),(6,"x11 x20 merge0 r00"),(8,"r10"),(10,"x21 merge1 r01 r20"),(11,"r30 r11"))
+AFTER=("x02","r40","r21","x12 x03","r31","x13","r41","x22 merge2 r02","r12","x23 merge3 r03","r22","r13","r32","r23","r42","r33","r43")
+
+def mega(table,queries,keys,values,output_gradient):
     V=lambda *sh,dt=BF: pltpu.VMEM(sh,dt)
     vm=pl.BlockSpec(memory_space=pltpu.VMEM); anyspec=pl.BlockSpec(memory_space=pl.ANY)
     return pl.pallas_call(mega_kernel,
-        in_specs=[pl.BlockSpec(memory_space=pltpu.SMEM),vm,vm,vm,anyspec,anyspec],
+        in_specs=[pl.BlockSpec(memory_space=pltpu.SMEM),vm,vm,anyspec,anyspec],
         out_specs=[anyspec,vm,vm],
         out_shape=[jax.ShapeDtypeStruct((384,4096),BF)]+[jax.ShapeDtypeStruct((512,256),BF)]*2,
         scratch_shapes=[V(16,512,128)]*4+[V(8,512,128)]*2+[V(8,512,128)]*4+[V(4,2,2,256,128),V(8,1,128,dt=jnp.int32),pltpu.SMEM((8,1,128),jnp.int32)]
             +[V(384,4096),V(384,4096),V(10,2,128,512,dt=F32)]+[V(8,2,128,512)]*2+[V(8,128,512)]*4+[V(16,128,512)]*2
-            +[V(4,2,2,64,512),V(4,2,4,2,32,512),V(4,2,4,2,64,512),V(4,2,4,64,512),V(2,64,512,dt=F32),V(4,2,2,32,512),V(4,2,2,64,512)]
-            +[pltpu.SemaphoreType.DMA((NSEM,)),pltpu.SemaphoreType.DMA((NSEM,)),pltpu.SemaphoreType.DMA((6,))],
+            +[V(4,2,2,64,512),V(4,2,4,2,32,512),V(4,2,4,2,64,512),V(4,2,4,64,512),V(4,2,64,512,dt=F32),V(4,2,2,32,512),V(4,2,2,64,512)]
+            +[pltpu.SemaphoreType.DMA((NSEM,)),pltpu.SemaphoreType.DMA((NSEM,)),pltpu.SemaphoreType.DMA((6,)),pltpu.SMEM((48,),jnp.int32),V(1,128,dt=jnp.int32)],
         compiler_params=pltpu.CompilerParams(collective_id=0,has_side_effects=True,vmem_limit_bytes=67043328),
-        name="mega")(info,want,keys,values,queries,output_gradient)
-def wants(table):
-    hit=(table%8).reshape(9,1)==jnp.arange(8,dtype=jnp.int32)[None]
-    rows=jnp.max(jnp.where(hit,(table//8).reshape(9,1),0),axis=0)
-    return jnp.pad(rows,(0,120)).reshape(1,128)
+        name="mega")(table,keys,values,queries,output_gradient)
 def local(queries,keys,values,output_gradient,tile_block_table):
-    me=lax.axis_index("row")*8+lax.axis_index("col")
-    info=make_info(tile_block_table,me)
-    return mega(info,wants(tile_block_table),queries,keys,values,output_gradient)
+    return mega(tile_block_table,queries,keys,values,output_gradient)
 def solution(mesh):
     from jax.sharding import PartitionSpec as P
     s=P(("row","col"),None)

time: 230 us -> 204 us (0.89)
  Pallas kernels: 221 us -> 198 us
    pallas_call x1, Pallas kernels: 221 us -> 198 us  [mega(): pl.pallas_call(mega_kernel, in_specs=[pl.BlockSpec(memory_space=pltpu.SME...]
where the time goes in v3:
time: 204 us
  Pallas kernels  198 us (97%)
  local copies, waits for them, and re-layouts  5.38 us (3%)
    pallas_call x1, Pallas kernels, mega(): pl.pallas_call(mega_kernel, in_specs=[pl.BlockSpec(memory_space=pltpu.SME...  198 us
    unnamed x7, local copies, waits for them, and re-layouts  5.38 us

profile of v3, /device:TPU:0, one launch (start us, length us, event | category | flops | bytes accessed | tf_op | source)
XLA Modules:
  0.0 203.7 jit_solution(11545589467003147631)
XLA Ops:
  0.6 197.7 %mega.1 = (bf16[384,4096]{1,0:T(8,128)(2,1)}, bf16[512,256]{1,0:T(8,128)(2,1)}, bf16[512,256]{1,0:T(8,128)(2,1)}) custom-call(s32[3,3]{1,0:T(4,128)} %table_ref.1, bf16[512,256]{1,0:T(8,128)(2,1)} %k_ref.1, bf16[512,256]{1,0:T(8,128)(2,1)} %v_ref.1, bf16[384,4096]{1,0:T(8,128)(2,1)} %q_hbm.1, bf16[384,4096]{1,0:T(8,128)(2,1)} %do_hbm.1), custom_call_target="tpu_custom_call" | custom-call | tf_op jit(solution)/shard_map/mega/pallas_call | solution.py:346
  198.3 0.0 copy-start.1
  198.3 0.0 copy-start
  198.3 4.0 %copy.11 = bf16[384,4096]{1,0:T(8,128)(2,1)} copy(bf16[384,4096]{1,0:T(8,128)(2,1)} %get-tuple-element.6) | data formatting | bytes 6291456
  202.3 0.0 copy-done.1
  202.3 0.7 copy.12
  203.0 0.0 copy-done
  203.0 0.7 copy.13
Async XLA Ops:
  198.3 4.0 %copy-start.1 = (bf16[512,256]{1,0:T(8,128)(2,1)S(1)}, bf16[512,256]{1,0:T(8,128)(2,1)}, u32[]{:S(2)}) copy-start(bf16[512,256]{1,0:T(8,128)(2,1)} %get-tuple-element.7) | copy-start | bytes 786436
  198.3 4.7 %copy-start = (bf16[512,256]{1,0:T(8,128)(2,1)S(1)}, bf16[512,256]{1,0:T(8,128)(2,1)}, u32[]{:S(2)}) copy-start(bf16[512,256]{1,0:T(8,128)(2,1)} %get-tuple-element.8) | copy-start | bytes 786436

commit v4 on v3

--- a/solution.py
+++ b/solution.py
@@ -334,9 +334,9 @@
         rows.append(" ".join(f"{nm}{k}" for k,o in enumerate(offsets) for i,nm in enumerate(names) if i==t-o))
     return rows
 STEPS=("s0","s1","s2","s3","s4","s5","s6","pick","e0","e1","e2")
-BEFORE=stagger((0,1,5,6),11,STEPS)+["e21"]
+BEFORE=stagger((0,1,8,9),11,STEPS)+["e21"]
 ZERO_AFTER=BEFORE[4]
-UNDER0=((0,"s62 pick2 e02"),(1,"s53"),(2,"s63 pick3 e12 e03"),(5,"e13"),(11,"e22 e23"))
+UNDER0=((0,"s32 s23"),(1,"s42 s33"),(2,"s52 s43"),(3,"s62 s53 pick2 e02"),(5,"s63 pick3 e12 e03"),(7,"e13"),(11,"e22 e23"))
 UNDER1=((0,"x00"),(2,"x10 x01"),(6,"x11 x20 merge0 r00"),(8,"r10"),(10,"x21 merge1 r01 r20"),(11,"r30 r11"))
 AFTER=("x02","r40","r21","x12 x03","r31","x13","r41","x22 merge2 r02","r12","x23 merge3 r03","r22","r13","r32","r23","r42","r33","r43")
 

time: 204 us -> 202 us (level)
  no operation moved by 1% of the time
where the time goes in v4:
time: 202 us
  Pallas kernels  196 us (97%)
  local copies, waits for them, and re-layouts  5.38 us (3%)
    pallas_call x1, Pallas kernels, mega(): pl.pallas_call(mega_kernel, in_specs=[pl.BlockSpec(memory_space=pltpu.SME...  196 us
    unnamed x7, local copies, waits for them, and re-layouts  5.38 us

profile of v4, /device:TPU:0, one launch (start us, length us, event | category | flops | bytes accessed | tf_op | source)
XLA Modules:
  0.0 201.7 jit_solution(3547576743418788308)
XLA Ops:
  0.6 195.7 %mega.1 = (bf16[384,4096]{1,0:T(8,128)(2,1)}, bf16[512,256]{1,0:T(8,128)(2,1)}, bf16[512,256]{1,0:T(8,128)(2,1)}) custom-call(s32[3,3]{1,0:T(4,128)} %table_ref.1, bf16[512,256]{1,0:T(8,128)(2,1)} %k_ref.1, bf16[512,256]{1,0:T(8,128)(2,1)} %v_ref.1, bf16[384,4096]{1,0:T(8,128)(2,1)} %q_hbm.1, bf16[384,4096]{1,0:T(8,128)(2,1)} %do_hbm.1), custom_call_target="tpu_custom_call" | custom-call | tf_op jit(solution)/shard_map/mega/pallas_call | solution.py:346
  196.3 0.0 copy-start.1
  196.4 0.0 copy-start
  196.4 4.0 %copy.11 = bf16[384,4096]{1,0:T(8,128)(2,1)} copy(bf16[384,4096]{1,0:T(8,128)(2,1)} %get-tuple-element.6) | data formatting | bytes 6291456
  200.3 0.0 copy-done.1
  200.3 0.7 copy.12
  201.0 0.0 copy-done
  201.0 0.7 copy.13
Async XLA Ops:
  196.3 4.0 %copy-start.1 = (bf16[512,256]{1,0:T(8,128)(2,1)S(1)}, bf16[512,256]{1,0:T(8,128)(2,1)}, u32[]{:S(2)}) copy-start(bf16[512,256]{1,0:T(8,128)(2,1)} %get-tuple-element.7) | copy-start | bytes 786436
  196.4 4.7 %copy-start = (bf16[512,256]{1,0:T(8,128)(2,1)S(1)}, bf16[512,256]{1,0:T(8,128)(2,1)}, u32[]{:S(2)}) copy-start(bf16[512,256]{1,0:T(8,128)(2,1)} %get-tuple-element.8) | copy-start | bytes 786436
